TPU v7x, 32 devices: a whole 2x2x4 slice. The times are simulated.
32 devices in a mesh: section: 4 (over x, core), paths: 8 (over z, y).
Axes of the slice: x: 2, y: 2, z: 4, core: 2. Of those that a mesh axis runs over, the one named last changes fastest.
Arguments:
- normal_draws: float32 [8, 60, 8192], P('section', None, 'paths'), may hold values from -6 to 6
- cholesky: float32 [8, 8, 60, 60], P('section', 'paths'), as said below
- log_spot: float32 [60], replicated, may hold values from -0.2 to 0.2
- owner: int32 [8], replicated, may hold values from 0 to 7
- trade_factor: int32 [4096], replicated, may hold values from 0 to 59
- trade_set: int32 [4096], replicated, may hold values from 0 to 511
- notional: float32 [4096], replicated, may hold values from -5 to 5
- strike: float32 [4096], replicated, may hold values from 0.8 to 1.25
Outputs:
- exposure: float32 [8, 512], P('section')
Inputs may be any that keep to these rules, and one draw needn't show every extreme that they name: `cholesky`: each block is lower triangular with a positive diagonal.
All inputs are finite; a program needn't handle non-finite values.
Results may differ from a plain program's by a relative error of at most 0.0001.
Values sent between devices are 32-bit elements; how exact they have to be, the bound alone decides.
No kernel may reach another device: no remote copies, remote signals or barrier semaphores. Data moves between devices by JAX's collectives and lax.ppermute only.
A program may use at most 64 MiB of HBM per device.

v0:
```python
import functools

import jax
import jax.numpy as jnp
from jax import lax
from jax.experimental import pallas as pl
from jax.experimental.pallas import tpu as pltpu
from jax.sharding import PartitionSpec as P

SETS = 512
LANES = 128
BLOCKS = SETS // LANES
CHUNK = 2 * LANES
ROWS = 32
GROUPS = 16
UNROLL = 4


def summed(part, axis):
    size = lax.axis_size(axis)
    if size & (size - 1):
        return lax.psum(part, axis)
    distance = 1
    while distance < size:
        part = part + lax.ppermute(part, axis, [(i, i ^ distance) for i in range(size)])
        distance *= 2
    return part


def pieces(value):
    first = value.astype(jnp.bfloat16).astype(jnp.float32)
    rest = value - first
    second = rest.astype(jnp.bfloat16).astype(jnp.float32)
    return first, second, rest - second


def dot_last(a, b):
    return lax.dot_general(a, b, (((1,), (1,)), ((), ())), preferred_element_type=jnp.float32)


def iota(shape, dim):
    return lax.broadcasted_iota(jnp.int32, shape, dim)


def table_kernel(
    factor_ref, set_ref, notional_ref, strike_ref,
    index_ref, level_ref, weight_ref, offset_ref, place_ref, count_ref,
    before_ref, base_ref, table_ref,
):
    chunks = factor_ref.shape[0] // 2
    before_ref[...] = (iota((CHUNK, CHUNK), 0) < iota((CHUNK, CHUNK), 1)).astype(jnp.bfloat16)
    base_ref[...] = jnp.zeros_like(base_ref)
    table_ref[...] = jnp.zeros_like(table_ref)
    set_ids = iota((SETS, LANES), 0)
    row_ids = iota((ROWS, LANES), 0).astype(jnp.float32)

    def chunk(step, carry):
        masks, rows = [], []
        for half in range(2):
            masks.append(set_ids == set_ref[pl.ds(2 * step + half, 1), :])
        hot = jnp.concatenate([m.astype(jnp.float32).astype(jnp.bfloat16) for m in masks], axis=1)
        earlier = jnp.dot(hot, before_ref[...], preferred_element_type=jnp.float32)
        base = base_ref[...]
        for half in range(2):
            rank = jnp.sum(
                jnp.where(masks[half], earlier[:, half * LANES : (half + 1) * LANES] + base, 0.0),
                axis=0, keepdims=True,
            )
            here = row_ids == rank
            own = pl.ds(2 * step + half, 1)
            values = (
                (factor_ref[own, :].astype(jnp.float32),)
                + pieces(strike_ref[own, :])
                + pieces(notional_ref[own, :])
            )
            rows.append([jnp.where(here, v, 0.0) for v in values])
        parts = [
            jnp.concatenate([rows[0][i], rows[1][i]], axis=1).astype(jnp.bfloat16)
            for i in range(len(rows[0]))
        ]
        parts.append(jnp.ones((16, CHUNK), jnp.bfloat16))
        table_ref[...] += dot_last(jnp.concatenate(parts, axis=0), hot)
        last = earlier[:, CHUNK - 1 :] + masks[1][:, LANES - 1 :].astype(jnp.float32)
        base_ref[...] = base + jnp.broadcast_to(last, (SETS, LANES))
        return carry

    lax.fori_loop(0, chunks, chunk, 0)
    table = table_ref[...]
    counts = table[7 * ROWS : 7 * ROWS + 1, :]
    base = base_ref[...]
    places = []
    for block in range(BLOCKS):
        own = counts[:, block * LANES : (block + 1) * LANES]
        mine = iota((SETS, LANES), 1) + block * LANES
        ahead = (base > own) | ((base == own) & (set_ids < mine))
        places.append(jnp.sum(jnp.where(ahead, 1.0, 0.0), axis=0, keepdims=True))
    place = jnp.concatenate(places, axis=1)
    moved = (iota((SETS, SETS), 0).astype(jnp.float32) == place).astype(jnp.float32)
    moved = moved.astype(jnp.bfloat16)
    place_ref[...] = moved
    table = dot_last(table[: 7 * ROWS, :].astype(jnp.bfloat16), moved)
    index = table[:ROWS, :].astype(jnp.int32)
    level = table[ROWS : 2 * ROWS] + (table[2 * ROWS : 3 * ROWS] + table[3 * ROWS : 4 * ROWS])
    weight = table[4 * ROWS : 5 * ROWS] + (table[5 * ROWS : 6 * ROWS] + table[6 * ROWS :])
    offset = -jnp.sum(level * weight, axis=0, keepdims=True)
    for block in range(BLOCKS):
        own = slice(block * LANES, (block + 1) * LANES)
        index_ref[pl.ds(block * ROWS, ROWS), :] = index[:, own]
        level_ref[pl.ds(block * ROWS, ROWS), :] = level[:, own]
        weight_ref[pl.ds(block * ROWS, ROWS), :] = weight[:, own]
        offset_ref[pl.ds(block, 1), :] = offset[:, own]
        most = jnp.max(jnp.where(place == float(block * LANES), counts, 0.0))
        count_ref[block] = most.astype(jnp.int32)


def tables(trade_factor, trade_set, notional, strike):
    lines = trade_factor.shape[0] // LANES
    packed = [a.reshape(lines, LANES) for a in (trade_factor, trade_set, notional, strike)]
    vmem = pl.BlockSpec(memory_space=pltpu.VMEM)
    grid_rows = (BLOCKS * ROWS, LANES)
    return pl.pallas_call(
        table_kernel,
        out_shape=(
            jax.ShapeDtypeStruct(grid_rows, jnp.int32),
            jax.ShapeDtypeStruct(grid_rows, jnp.float32),
            jax.ShapeDtypeStruct(grid_rows, jnp.float32),
            jax.ShapeDtypeStruct((BLOCKS, LANES), jnp.float32),
            jax.ShapeDtypeStruct((SETS, SETS), jnp.bfloat16),
            jax.ShapeDtypeStruct((BLOCKS,), jnp.int32),
        ),
        in_specs=[vmem] * 4,
        out_specs=(vmem,) * 5 + (pl.BlockSpec(memory_space=pltpu.SMEM),),
        scratch_shapes=[
            pltpu.VMEM((CHUNK, CHUNK), jnp.bfloat16),
            pltpu.VMEM((SETS, LANES), jnp.float32),
            pltpu.VMEM((7 * ROWS + 16, SETS), jnp.float32),
        ],
        cost_estimate=pl.CostEstimate(
            flops=2 * trade_factor.shape[0] * SETS * 500, transcendentals=0, bytes_accessed=1 << 20
        ),
        name="tables",
    )(*packed)


def picked(values, index):
    numbers = lax.GatherDimensionNumbers(
        offset_dims=(), collapsed_slice_dims=(1,), start_index_map=(1,),
        operand_batching_dims=(0,), start_indices_batching_dims=(0,),
    )
    return lax.gather(
        values, index[..., None], numbers, slice_sizes=(1, 1),
        mode=lax.GatherScatterMode.PROMISE_IN_BOUNDS,
    )


def exposure_kernel(
    count_ref, index_ref, strike_ref, weight_ref, offset_ref, place_ref, spot_ref, carry_ref, own_ref,
    factor_hbm, set_hbm, notional_hbm, strike_hbm,
    out_ref,
    level_ref, price_ref, sum_ref, net_ref, factor_s, set_s, notional_s, strike_s,
):
    dates, factors, paths = own_ref.shape
    half = LANES // 2
    carried = carry_ref[...] + spot_ref[...]
    level_ref[...] = jnp.zeros_like(level_ref)
    for date in range(dates):
        level_ref[pl.ds(date * half, factors), :] = jnp.exp(carried + own_ref[date])
    groups = paths // 8
    price_ref[...] = jnp.transpose(level_ref[...]).reshape(groups, 8, LANES)
    sum_ref[...] = jnp.zeros_like(sum_ref)
    largest = count_ref[0]

    @pl.when(largest <= ROWS)
    def _():
        def some(step, carry):
            values = [price_ref[step * GROUPS + i] for i in range(GROUPS)]
            for block in range(BLOCKS):
                start = jnp.broadcast_to(offset_ref[pl.ds(block, 1), :], (8, LANES))

                def rows(r, nets):
                    for u in range(UNROLL):
                        at = pl.ds(block * ROWS + r * UNROLL + u, 1)
                        index = jnp.broadcast_to(index_ref[at, :], (8, LANES))
                        strike = jnp.broadcast_to(strike_ref[at, :], (8, LANES))
                        weight = jnp.broadcast_to(weight_ref[at, :], (8, LANES))
                        nets = tuple(
                            tuple(
                                net + weight * jnp.maximum(picked(v, index + date * half), strike)
                                for net, v in zip(nets[date], values)
                            )
                            for date in range(dates)
                        )
                    return nets

                nets = lax.fori_loop(
                    0, (count_ref[block] + UNROLL - 1) // UNROLL, rows, ((start,) * GROUPS,) * dates
                )
                for date in range(dates):
                    sum_ref[date, block] += sum(jnp.maximum(net, 0.0) for net in nets[date])
            return carry

        lax.fori_loop(0, groups // GROUPS, some, 0)
        total = jnp.concatenate(
            [
                jnp.concatenate(
                    [jnp.sum(sum_ref[date, block], axis=0, keepdims=True) for block in range(BLOCKS)], axis=1
                )
                for date in range(dates)
            ]
            + [jnp.zeros((16 - dates, SETS), jnp.float32)],
            axis=0,
        )
        place = place_ref[...]
        parts = [jnp.dot(p.astype(jnp.bfloat16), place, preferred_element_type=jnp.float32) for p in pieces(total)]
        out_ref[...] = (parts[0] + (parts[1] + parts[2]))[:dates]

    @pl.when(largest > ROWS)
    def _():
        pltpu.sync_copy(factor_hbm, factor_s)
        pltpu.sync_copy(set_hbm, set_s)
        pltpu.sync_copy(notional_hbm, notional_s)
        pltpu.sync_copy(strike_hbm, strike_s)
        for date in range(dates):
            net_ref[...] = jnp.zeros_like(net_ref)

            def trade(t, carry):
                price = level_ref[pl.ds(factor_s[t] + date * half, 1), :]
                at = pl.ds(set_s[t], 1)
                net_ref[at, :] += notional_s[t] * jnp.maximum(price - strike_s[t], 0.0)
                return carry

            lax.fori_loop(0, factor_s.shape[0], trade, 0)
            ones = jnp.ones((8, paths), jnp.float32)
            out_ref[pl.ds(date, 1), :] = lax.dot_general(
                ones, jnp.maximum(net_ref[...], 0.0), (((1,), (1,)), ((), ())),
                precision=lax.Precision.HIGHEST, preferred_element_type=jnp.float32,
            )[:1]


def exposures(built, log_spot, before, own, trades):
    index, strike, weight, offset, place, count = built
    dates, factors, paths = own.shape
    vmem, hbm = pl.BlockSpec(memory_space=pltpu.VMEM), pl.BlockSpec(memory_space=pl.ANY)
    number = trades[0].shape
    return pl.pallas_call(
        exposure_kernel,
        out_shape=jax.ShapeDtypeStruct((dates, SETS), jnp.float32),
        in_specs=[pl.BlockSpec(memory_space=pltpu.SMEM)] + [vmem] * 8 + [hbm] * 4,
        out_specs=vmem,
        scratch_shapes=[
            pltpu.VMEM((LANES, paths), jnp.float32),
            pltpu.VMEM((paths // 8, 8, LANES), jnp.float32),
            pltpu.VMEM((dates, BLOCKS, 8, LANES), jnp.float32),
            pltpu.VMEM((SETS, paths), jnp.float32),
            pltpu.SMEM(number, jnp.int32),
            pltpu.SMEM(number, jnp.int32),
            pltpu.SMEM(number, jnp.float32),
            pltpu.SMEM(number, jnp.float32),
        ],
        name="exposures",
    )(count, index, strike, weight, offset, place, log_spot[:, None], before, own, *trades)


def shards(normal_draws, cholesky, log_spot, owner, trade_factor, trade_set, notional, strike):
    local_dates = normal_draws.shape[0]
    section, sections = lax.axis_index("section"), lax.axis_size("section")
    trades = (trade_factor, trade_set, notional, strike)
    built = tables(*trades)
    owners_here = lax.dynamic_slice_in_dim(owner, section * local_dates, local_dates)
    mine = (owners_here == lax.axis_index("paths"))[:, None, None]
    blocks = summed(jnp.where(mine, cholesky[:, 0], 0.0), "paths")
    running = jnp.zeros(normal_draws.shape[1:], jnp.float32)
    prefixes = []
    for date in range(local_dates):
        increment = jnp.dot(
            blocks[date],
            normal_draws[date],
            precision=lax.Precision.HIGHEST,
            preferred_element_type=jnp.float32,
        )
        running = running + increment
        prefixes.append(running)
    gathered = lax.all_gather(running, "section")
    earlier = (jnp.arange(sections) < section)[:, None, None]
    before = jnp.sum(jnp.where(earlier, gathered, 0.0), axis=0)
    sums = exposures(built, log_spot, before, jnp.stack(prefixes, axis=0), trades)
    totals = summed(sums, "paths")
    return totals / (normal_draws.shape[2] * lax.axis_size("paths"))


def solution(mesh):
    placed = (P("section", None, "paths"), P("section", "paths", None, None)) + (P(),) * 6
    return jax.shard_map(
        shards, mesh=mesh, in_specs=placed, out_specs=P("section", None), check_vma=False
    )
```

profile of v0, /device:TPU:0, one launch (start us, length us, event | category | flops | bytes accessed | tf_op | source)
XLA Modules:
  0.0 77.2 jit_solution(2375002132463738625)
XLA Ops:
  0.0 0.0 copy-start.2
  0.0 0.7 copy-done.2
  0.7 0.1 dynamic-slice_compare_fusion
  0.7 0.9 %bitcast_select_fusion = f32[2,60,60]{2,0,1:T(2,128)S(1)} fusion(f32[2,1,60,60]{3,1,2,0:T(1,128)} %param.9, pred[2]{0:T(512)(128)(4,1)S(1)} %dynamic-slice_compare_fusion), kind=kLoop, calls=%fused_computation.7 | loop fusion | flops 7200 | bytes 57602 | tf_op jit(solution)/shard_map/jit(_where)/select_n | solution.py:271
  1.7 0.0 copy-start
  1.7 3.1 %collective-permute-start = (f32[2,60,60]{2,0,1:T(2,128)S(1)}, f32[2,60,60]{2,0,1:T(2,128)S(1)}, u32[]{:S(2)}, u32[]{:S(2)}) collective-permute-start(f32[2,60,60]{2,0,1:T(2,128)S(1)} %bitcast_select_fusion), channel_id=1, source_target_pairs={{0,1},{1,0},{2,3},{3,2},{4,5},{5,4},{6,7},{7,6},{8,9},{9,8},{10,11... | collective-permute-start | bytes 86408 | tf_op jit(solution)/shard_map/ppermute | solution.py:25
  4.7 1.7 %fusion.6 = (f32[1,60,1024]{2,0,1:T(1,128)S(1)}, f32[1,60,1024]{2,0,1:T(1,128)S(1)}) fusion(f32[2,60,1024]{2,0,1:T(2,128)} %param.8), kind=kLoop, calls=%fused_computation.15 | loop fusion | bytes 983040 | tf_op jit(solution)/shard_map/slice | solution.py:277
  6.4 0.5 collective-permute-done
  6.9 0.0 copy-done
  6.9 0.1 fusion.8
  7.0 2.1 %collective-permute-start.1 = (f32[2,60,60]{2,0,1:T(2,128)S(1)}, f32[2,60,60]{2,0,1:T(2,128)S(1)}, u32[]{:S(2)}, u32[]{:S(2)}) collective-permute-start(f32[2,60,60]{2,0,1:T(2,128)S(1)} %fusion.8), channel_id=1, source_target_pairs={{0,2},{1,3},{2,0},{3,1},{4,6},{5,7},{6,4},{7,5},{8,10},{9,11},{10,... | collective-permute-start | bytes 86408 | tf_op jit(solution)/shard_map/ppermute | solution.py:25
  9.2 10.9 %tables.1 = (s32[128,128]{1,0:T(8,128)}, f32[128,128]{1,0:T(8,128)}, f32[128,128]{1,0:T(8,128)}, f32[4,128]{1,0:T(4,128)}, bf16[512,512]{1,0:T(8,128)(2,1)}, /*index=5*/s32[4]{0:T(128)}) custom-call(s32[32,128]{1,0:T(8,128)} %bitcast.25, s32[32,128]{1,0:T(8,128)} %bitcast.26, f32[32,128]{1,0:T(8,128)} %bitcast.27, f32[32,128]{1,0:T(8,128)} %bitcast.28), custom_call_target="tpu_custom_call" | custom-call | flops 2097152000 | bytes 1048576 | tf_op jit(solution)/shard_map/tables/pallas_call | solution.py:121
  20.1 0.0 collective-permute-done.1
  20.2 2.6 %collective-permute-start.2 = (f32[2,60,60]{2,0,1:T(2,128)S(1)}, f32[2,60,60]{2,0,1:T(2,128)S(1)}, u32[]{:S(2)}, u32[]{:S(2)}) collective-permute-start(f32[2,60,60]{2,0,1:T(2,128)S(1)} %add.26), channel_id=1, source_target_pairs={{0,4},{1,5},{2,6},{3,7},{4,0},{5,1},{6,2},{7,3},{8,12},{9,13},{10,... | collective-permute-start | bytes 86408 | tf_op jit(solution)/shard_map/ppermute | solution.py:25
  22.8 0.0 copy-start.1
  22.8 0.7 copy-done.1
  23.5 0.7 copy.17.spot_ref
  24.2 1.4 %collective-permute-done.2 = f32[2,60,60]{2,0,1:T(2,128)S(1)} collective-permute-done((f32[2,60,60]{2,0,1:T(2,128)S(1)}, f32[2,60,60]{2,0,1:T(2,128)S(1)}, u32[]{:S(2)}, u32[]{:S(2)}) %collective-permute-start.2) | collective-permute-done | bytes 28832 | tf_op jit(solution)/shard_map/ppermute | solution.py:25
  25.7 0.4 fusion.1
  26.1 0.4 fusion
  26.4 10.3 %all-gather.1 = f32[4,60,1024]{2,1,0:T(8,128)S(1)} all-gather(f32[1,60,1024]{2,1,0:T(8,128)S(1)} %fusion), channel_id=2, replica_groups=mesh['section'=4,'paths'=8] {'section'}, dimensions={0}, use_global_device_ids=true | all-gather | bytes 1228800 | tf_op jit(solution)/shard_map/all_gather | solution.py:283
  36.8 0.8 %pad_maximum_fusion.own_ref = f32[2,60,1024]{2,1,0:T(8,128)} fusion(f32[1,60,1024]{2,1,0:T(8,128)S(1)} %fusion, f32[1,60,1024]{2,1,0:T(8,128)S(1)} %bitcast.24), kind=kLoop, calls=%fused_computation.3 | loop fusion | flops 122880 | bytes 983040 | tf_op jit(solution)/shard_map/stack | solution.py:286
  37.6 0.9 %select_reduce_fusion.carry_ref = f32[60,1024]{1,0:T(8,128)} fusion(f32[4,60,1024]{2,1,0:T(8,128)S(1)} %all-gather.1, pred[4]{0:T(512)(128)(4,1)S(1)} %iota_compare_fusion), kind=kLoop, calls=%fused_computation.2 | loop fusion | flops 430080 | bytes 1228804 | tf_op jit(solution)/shard_map/reduce_sum | solution.py:285
  38.5 25.5 %exposures.1 = f32[2,512]{1,0:T(2,128)} custom-call(s32[4]{0:T(128)} %get-tuple-element.11.count_ref, s32[128,128]{1,0:T(8,128)} %get-tuple-element.12.index_ref, f32[128,128]{1,0:T(8,128)} %get-tuple-element.13.strike_ref, f32[128,128]{1,0:T(8,128)} %get-tuple-element.14.weight_ref, f32[4,128]{1,0:T(4,128)} %get-tuple-element.15.offset_ref, ...), custom_call_target="tpu_custom_call" | custom-call | tf_op jit(solution)/shard_map/exposures/pallas_call | solution.py:245
  64.0 1.5 %collective-permute-start.3 = (f32[2,512]{1,0:T(2,128)}, f32[2,512]{1,0:T(2,128)S(1)}, u32[]{:S(2)}, u32[]{:S(2)}) collective-permute-start(f32[2,512]{1,0:T(2,128)} %exposures.1), channel_id=1, source_target_pairs={{0,1},{1,0},{2,3},{3,2},{4,5},{5,4},{6,7},{7,6},{8,9},{9,8},{10,11... | collective-permute-start | bytes 12296 | tf_op jit(solution)/shard_map/ppermute | solution.py:25
  65.5 2.3 %collective-permute-done.3 = f32[2,512]{1,0:T(2,128)S(1)} collective-permute-done((f32[2,512]{1,0:T(2,128)}, f32[2,512]{1,0:T(2,128)S(1)}, u32[]{:S(2)}, u32[]{:S(2)}) %collective-permute-start.3) | collective-permute-done | bytes 4128 | tf_op jit(solution)/shard_map/ppermute | solution.py:25
  67.8 0.7 add.29
  68.5 0.0 collective-permute-start.4
  68.5 3.6 %collective-permute-done.4 = f32[2,512]{1,0:T(2,128)S(1)} collective-permute-done((f32[2,512]{1,0:T(2,128)S(1)}, f32[2,512]{1,0:T(2,128)S(1)}, u32[]{:S(2)}, u32[]{:S(2)}) %collective-permute-start.4) | collective-permute-done | bytes 4128 | tf_op jit(solution)/shard_map/ppermute | solution.py:25
  72.1 2.1 %collective-permute-start.5 = (f32[2,512]{1,0:T(2,128)S(1)}, f32[2,512]{1,0:T(2,128)S(1)}, u32[]{:S(2)}, u32[]{:S(2)}) collective-permute-start(f32[2,512]{1,0:T(2,128)S(1)} %add.30), channel_id=1, source_target_pairs={{0,4},{1,5},{2,6},{3,7},{4,0},{5,1},{6,2},{7,3},{8,12},{9,13},{10,... | collective-permute-start | bytes 12296 | tf_op jit(solution)/shard_map/ppermute | solution.py:25
  74.1 2.5 %collective-permute-done.5 = f32[2,512]{1,0:T(2,128)S(1)} collective-permute-done((f32[2,512]{1,0:T(2,128)S(1)}, f32[2,512]{1,0:T(2,128)S(1)}, u32[]{:S(2)}, u32[]{:S(2)}) %collective-permute-start.5) | collective-permute-done | bytes 4128 | tf_op jit(solution)/shard_map/ppermute | solution.py:25
  76.6 0.6 add_multiply_fusion
  (5 shorter events, 0.1 us)
Async XLA Ops:
  0.0 0.7 copy-start.2
  1.7 5.3 %copy-start = (f32[2,1,60,60]{3,1,2,0:T(1,128)S(1)}, f32[2,1,60,60]{3,1,2,0:T(1,128)}, u32[]{:S(2)}) copy-start(f32[2,1,60,60]{3,1,2,0:T(1,128)} %param.9) | copy-start | bytes 86404
  1.7 5.3 %collective-permute-start = (f32[2,60,60]{2,0,1:T(2,128)S(1)}, f32[2,60,60]{2,0,1:T(2,128)S(1)}, u32[]{:S(2)}, u32[]{:S(2)}) collective-permute-start(f32[2,60,60]{2,0,1:T(2,128)S(1)} %bitcast_select_fusion), channel_id=1, source_target_pairs={{0,1},{1,0},{2,3},{3,2},{4,5},{5,4},{6,7},{7,6},{8,9},{9,8},{10,11... | collective-permute-start | bytes 86408 | tf_op jit(solution)/shard_map/ppermute | solution.py:25
  7.0 13.1 %collective-permute-start.1 = (f32[2,60,60]{2,0,1:T(2,128)S(1)}, f32[2,60,60]{2,0,1:T(2,128)S(1)}, u32[]{:S(2)}, u32[]{:S(2)}) collective-permute-start(f32[2,60,60]{2,0,1:T(2,128)S(1)} %fusion.8), channel_id=1, source_target_pairs={{0,2},{1,3},{2,0},{3,1},{4,6},{5,7},{6,4},{7,5},{8,10},{9,11},{10,... | collective-permute-start | bytes 86408 | tf_op jit(solution)/shard_map/ppermute | solution.py:25
  20.2 5.4 %collective-permute-start.2 = (f32[2,60,60]{2,0,1:T(2,128)S(1)}, f32[2,60,60]{2,0,1:T(2,128)S(1)}, u32[]{:S(2)}, u32[]{:S(2)}) collective-permute-start(f32[2,60,60]{2,0,1:T(2,128)S(1)} %add.26), channel_id=1, source_target_pairs={{0,4},{1,5},{2,6},{3,7},{4,0},{5,1},{6,2},{7,3},{8,12},{9,13},{10,... | collective-permute-start | bytes 86408 | tf_op jit(solution)/shard_map/ppermute | solution.py:25
  22.8 0.7 copy-start.1
  64.0 3.8 %collective-permute-start.3 = (f32[2,512]{1,0:T(2,128)}, f32[2,512]{1,0:T(2,128)S(1)}, u32[]{:S(2)}, u32[]{:S(2)}) collective-permute-start(f32[2,512]{1,0:T(2,128)} %exposures.1), channel_id=1, source_target_pairs={{0,1},{1,0},{2,3},{3,2},{4,5},{5,4},{6,7},{7,6},{8,9},{9,8},{10,11... | collective-permute-start | bytes 12296 | tf_op jit(solution)/shard_map/ppermute | solution.py:25
  68.5 3.6 %collective-permute-start.4 = (f32[2,512]{1,0:T(2,128)S(1)}, f32[2,512]{1,0:T(2,128)S(1)}, u32[]{:S(2)}, u32[]{:S(2)}) collective-permute-start(f32[2,512]{1,0:T(2,128)S(1)} %add.29), channel_id=1, source_target_pairs={{0,2},{1,3},{2,0},{3,1},{4,6},{5,7},{6,4},{7,5},{8,10},{9,11},{10,... | collective-permute-start | bytes 12296 | tf_op jit(solution)/shard_map/ppermute | solution.py:25
  72.1 4.5 %collective-permute-start.5 = (f32[2,512]{1,0:T(2,128)S(1)}, f32[2,512]{1,0:T(2,128)S(1)}, u32[]{:S(2)}, u32[]{:S(2)}) collective-permute-start(f32[2,512]{1,0:T(2,128)S(1)} %add.30), channel_id=1, source_target_pairs={{0,4},{1,5},{2,6},{3,7},{4,0},{5,1},{6,2},{7,3},{8,12},{9,13},{10,... | collective-permute-start | bytes 12296 | tf_op jit(solution)/shard_map/ppermute | solution.py:25
where the time goes:
time: 77.6 us; the launch traced here: 77.2 us
  Pallas kernels  36.4 us (47%)
  starting transfers between devices  11.4 us (15%)
  blocking collectives  10.3 us (13%)
  waiting for transfers between devices  10.2 us (13%)
  other arithmetic  4.16 us (5%)
  local copies, waits for them, and re-layouts  3.77 us (5%)
    pallas_call x1, Pallas kernels, exposures(): pl.pallas_call(exposure_kernel, out_shape=jax.ShapeDtypeStruct((dates, SE...  25.5 us
    ppermute x6, starting transfers between devices, summed(): lax.ppermute(part, axis, [(i, i ^ distance) for i in range(size)])  11.4 us
    pallas_call x1, Pallas kernels, tables(): pl.pallas_call(table_kernel, out_shape=(jax.ShapeDtypeStruct(grid_rows, j...  10.9 us
    all_gather x1, blocking collectives, shards(): gathered = lax.all_gather(running, 'section')  10.3 us
    ppermute x6, waiting for transfers between devices, summed(): lax.ppermute(part, axis, [(i, i ^ distance) for i in range(size)])  10.2 us
    slice x1, local copies, waits for them, and re-layouts, shards(): normal_draws[date]  1.71 us
  transfers between devices with their start and end apart: 6, of which 5 were waited for; matrix products, arithmetic and copies ran while one was open for 3% of the time, Pallas kernels for 14%

commit v1 on v0

v1 whole, which is shorter than its diff:
```python
import functools

import jax
import jax.numpy as jnp
from jax import lax
from jax.experimental import pallas as pl
from jax.experimental.pallas import tpu as pltpu
from jax.sharding import PartitionSpec as P

SETS = 512
LANES = 128
LOW = 128.0
BLOCKS = SETS // LANES
CHUNK = 2 * LANES
ROWS = 32
GROUP = 16
UNROLL = 2


def summed(part, axis):
    size = lax.axis_size(axis)
    if size & (size - 1):
        return lax.psum(part, axis)
    distance = 1
    while distance < size:
        part = part + lax.ppermute(part, axis, [(i, i ^ distance) for i in range(size)])
        distance *= 2
    return part


def pieces(value):
    first = value.astype(jnp.bfloat16).astype(jnp.float32)
    rest = value - first
    second = rest.astype(jnp.bfloat16).astype(jnp.float32)
    return first, second, rest - second


def dot_last(a, b):
    return lax.dot_general(a, b, (((1,), (1,)), ((), ())), preferred_element_type=jnp.float32)


def iota(shape, dim):
    return lax.broadcasted_iota(jnp.int32, shape, dim)


def table_kernel(
    factor_ref, set_ref, notional_ref, level_ref,
    index_ref, strike_ref, weight_ref, place_ref, count_ref,
    before_ref, base_ref, table_ref,
):
    chunks = factor_ref.shape[0] // 2
    before_ref[...] = (iota((CHUNK, CHUNK), 0) < iota((CHUNK, CHUNK), 1)).astype(jnp.bfloat16)
    base_ref[...] = jnp.zeros_like(base_ref)
    table_ref[...] = jnp.zeros_like(table_ref)
    set_ids = iota((SETS, LANES), 0)
    row_ids = iota((ROWS, LANES), 0).astype(jnp.float32)

    def chunk(step, carry):
        masks, rows = [], []
        for half in range(2):
            masks.append(set_ids == set_ref[pl.ds(2 * step + half, 1), :])
        hot = jnp.concatenate([m.astype(jnp.float32).astype(jnp.bfloat16) for m in masks], axis=1)
        earlier = jnp.dot(hot, before_ref[...], preferred_element_type=jnp.float32)
        base = base_ref[...]
        for half in range(2):
            rank = jnp.sum(
                jnp.where(masks[half], earlier[:, half * LANES : (half + 1) * LANES] + base, 0.0),
                axis=0, keepdims=True,
            )
            here = row_ids == rank
            own = pl.ds(2 * step + half, 1)
            values = (
                (factor_ref[own, :].astype(jnp.float32),)
                + pieces(level_ref[own, :])
                + pieces(notional_ref[own, :])
            )
            rows.append([jnp.where(here, v, 0.0) for v in values])
        parts = [
            jnp.concatenate([rows[0][i], rows[1][i]], axis=1).astype(jnp.bfloat16)
            for i in range(len(rows[0]))
        ]
        parts.append(jnp.ones((16, CHUNK), jnp.bfloat16))
        table_ref[...] += dot_last(jnp.concatenate(parts, axis=0), hot)
        last = earlier[:, CHUNK - 1 :] + masks[1][:, LANES - 1 :].astype(jnp.float32)
        base_ref[...] = base + jnp.broadcast_to(last, (SETS, LANES))
        return carry

    lax.fori_loop(0, chunks, chunk, 0, unroll=4)
    table = table_ref[...]
    counts = table[7 * ROWS : 7 * ROWS + 1, :]
    base = base_ref[...]
    places = []
    for block in range(BLOCKS):
        own = counts[:, block * LANES : (block + 1) * LANES]
        mine = iota((SETS, LANES), 1) + block * LANES
        ahead = (base > own) | ((base == own) & (set_ids < mine))
        places.append(jnp.sum(jnp.where(ahead, 1.0, 0.0), axis=0, keepdims=True))
    place = jnp.concatenate(places, axis=1)
    moved = (iota((SETS, SETS), 0).astype(jnp.float32) == place).astype(jnp.float32)
    moved = moved.astype(jnp.bfloat16)
    place_ref[...] = moved
    table = dot_last(table[: 7 * ROWS, :].astype(jnp.bfloat16), moved)
    index = table[:ROWS, :].astype(jnp.int32)
    strike = table[ROWS : 2 * ROWS] + (table[2 * ROWS : 3 * ROWS] + table[3 * ROWS : 4 * ROWS])
    weight = table[4 * ROWS : 5 * ROWS] + (table[5 * ROWS : 6 * ROWS] + table[6 * ROWS : 7 * ROWS])
    for block in range(BLOCKS):
        own = slice(block * LANES, (block + 1) * LANES)
        index_ref[:, block, :] = index[:, own]
        strike_ref[:, block, :] = strike[:, own]
        weight_ref[:, block, :] = weight[:, own]
    exact = jnp.concatenate([(counts - LOW * jnp.floor(counts / LOW)), jnp.floor(counts / LOW)] + [jnp.zeros((14, SETS), jnp.float32)], axis=0)
    ordered = dot_last(exact.astype(jnp.bfloat16), moved)
    count_ref[...] = (ordered[:1] + LOW * ordered[1:2]).astype(jnp.int32)


def tables(trade_factor, trade_set, notional, strike):
    lines = trade_factor.shape[0] // LANES
    packed = [a.reshape(lines, LANES) for a in (trade_factor, trade_set, notional, strike)]
    vmem = pl.BlockSpec(memory_space=pltpu.VMEM)
    grid_rows = (ROWS, BLOCKS, LANES)
    return pl.pallas_call(
        table_kernel,
        out_shape=(
            jax.ShapeDtypeStruct(grid_rows, jnp.int32),
            jax.ShapeDtypeStruct(grid_rows, jnp.float32),
            jax.ShapeDtypeStruct(grid_rows, jnp.float32),
            jax.ShapeDtypeStruct((SETS, SETS), jnp.bfloat16),
            jax.ShapeDtypeStruct((1, SETS), jnp.int32),
        ),
        in_specs=[vmem] * 4,
        out_specs=(vmem,) * 5,
        scratch_shapes=[
            pltpu.VMEM((CHUNK, CHUNK), jnp.bfloat16),
            pltpu.VMEM((SETS, LANES), jnp.float32),
            pltpu.VMEM((7 * ROWS + 16, SETS), jnp.float32),
        ],
        cost_estimate=pl.CostEstimate(
            flops=2 * trade_factor.shape[0] * SETS * 500, transcendentals=0, bytes_accessed=1 << 20
        ),
        name="tables",
    )(*packed)


def over_sublanes(nets):
    row = iota((8, LANES), 0)
    for bit in (4, 2, 1):
        low = (row & bit) == 0
        nets = [
            jnp.where(low, a, pltpu.roll(b, bit, 0)) + jnp.where(low, pltpu.roll(a, 8 - bit, 0), b)
            for a, b in zip(nets[: len(nets) // 2], nets[len(nets) // 2 :])
        ]
    return nets[0]


def exposure_kernel(
    count_ref, index_ref, strike_ref, weight_ref, place_ref, spot_ref, carry_ref, own_ref,
    factor_hbm, set_hbm, notional_hbm, strike_hbm,
    out_ref,
    level_ref, price_ref, sum_ref, net_ref, factor_s, set_s, notional_s, strike_s,
):
    dates, factors, paths = own_ref.shape
    tiles = paths // LANES
    carried = carry_ref[...] + spot_ref[...]
    for date in range(dates):
        level = jnp.exp(carried + own_ref[date])
        level_ref[date] = level
        price_ref[:, date] = level.reshape(factors, tiles, LANES)
    largest = count_ref[0]

    @pl.when(largest <= ROWS)
    def _():
        def group(step, carry):
            first = step * GROUP

            def rows(r, nets):
                nets = [list(n) for n in nets]
                base = r * (UNROLL * SETS) + first
                for u in range(UNROLL):
                    for j in range(GROUP):
                        slot = base + u * SETS + j
                        index, strike, weight = index_ref[slot], strike_ref[slot], weight_ref[slot]
                        for date in range(dates):
                            price = price_ref[index, date]
                            nets[date][j] += weight * jnp.maximum(price - strike, 0.0)
                return tuple(tuple(n) for n in nets)

            zero = jnp.zeros((tiles, LANES), jnp.float32)
            nets = lax.fori_loop(
                0, (count_ref[first] + UNROLL - 1) // UNROLL, rows, ((zero,) * GROUP,) * dates
            )
            for date in range(dates):
                for part in range(GROUP // 8):
                    eight = [jnp.maximum(nets[date][part * 8 + i], 0.0) for i in range(8)]
                    at = pl.ds(pl.multiple_of(first + part * 8, 8), 8)
                    sum_ref[date, at, :] = over_sublanes(eight)
            return carry

        lax.fori_loop(0, SETS // GROUP, group, 0)
        ones = jnp.ones((8, LANES), jnp.bfloat16)
        lines = []
        for date in range(dates):
            lines.append(sum(dot_last(ones, p.astype(jnp.bfloat16)) for p in pieces(sum_ref[date]))[:1])
        total = jnp.concatenate(lines + [jnp.zeros((16 - dates, SETS), jnp.float32)], axis=0)
        place = place_ref[...]
        parts = [jnp.dot(p.astype(jnp.bfloat16), place, preferred_element_type=jnp.float32) for p in pieces(total)]
        out_ref[...] = (parts[0] + (parts[1] + parts[2]))[:dates]

    @pl.when(largest > ROWS)
    def _():
        pltpu.sync_copy(factor_hbm, factor_s)
        pltpu.sync_copy(set_hbm, set_s)
        pltpu.sync_copy(notional_hbm, notional_s)
        pltpu.sync_copy(strike_hbm, strike_s)

        def one_date(date, carry):
            net_ref[...] = jnp.zeros_like(net_ref)

            def trade(t, carry):
                price = level_ref[date, pl.ds(factor_s[t], 1), :]
                at = pl.ds(set_s[t], 1)
                net_ref[at, :] += notional_s[t] * jnp.maximum(price - strike_s[t], 0.0)
                return carry

            lax.fori_loop(0, factor_s.shape[0], trade, 0)
            sums = jnp.zeros((8, SETS), jnp.float32)
            ones = jnp.ones((8, LANES), jnp.bfloat16)
            for tile in range(tiles):
                for p in pieces(jnp.maximum(net_ref[:, tile * LANES : (tile + 1) * LANES], 0.0)):
                    sums += dot_last(ones, p.astype(jnp.bfloat16))
            out_ref[pl.ds(date, 1), :] = sums[:1]
            return carry

        lax.fori_loop(0, dates, one_date, 0)


def exposures(built, log_spot, before, own, trades):
    index, strike, weight, place, count = built
    dates, factors, paths = own.shape
    vmem, hbm = pl.BlockSpec(memory_space=pltpu.VMEM), pl.BlockSpec(memory_space=pl.ANY)
    number = trades[0].shape
    return pl.pallas_call(
        exposure_kernel,
        out_shape=jax.ShapeDtypeStruct((dates, SETS), jnp.float32),
        in_specs=[pl.BlockSpec(memory_space=pltpu.SMEM)] * 4 + [vmem] * 4 + [hbm] * 4,
        out_specs=vmem,
        scratch_shapes=[
            pltpu.VMEM((dates, factors, paths), jnp.float32),
            pltpu.VMEM((factors, dates, paths // LANES, LANES), jnp.float32),
            pltpu.VMEM((dates, SETS, LANES), jnp.float32),
            pltpu.VMEM((SETS, paths), jnp.float32),
            pltpu.SMEM(number, jnp.int32),
            pltpu.SMEM(number, jnp.int32),
            pltpu.SMEM(number, jnp.float32),
            pltpu.SMEM(number, jnp.float32),
        ],
        name="exposures",
    )(count.reshape(SETS), index.reshape(-1), strike.reshape(-1), weight.reshape(-1), place, log_spot[:, None], before, own, *trades)


def shards(normal_draws, cholesky, log_spot, owner, trade_factor, trade_set, notional, strike):
    local_dates = normal_draws.shape[0]
    section, sections = lax.axis_index("section"), lax.axis_size("section")
    trades = (trade_factor, trade_set, notional, strike)
    built = tables(*trades)
    owners_here = lax.dynamic_slice_in_dim(owner, section * local_dates, local_dates)
    mine = (owners_here == lax.axis_index("paths"))[:, None, None]
    blocks = summed(jnp.where(mine, cholesky[:, 0], 0.0), "paths")
    running = jnp.zeros(normal_draws.shape[1:], jnp.float32)
    prefixes = []
    for date in range(local_dates):
        increment = jnp.dot(
            blocks[date],
            normal_draws[date],
            precision=lax.Precision.HIGHEST,
            preferred_element_type=jnp.float32,
        )
        running = running + increment
        prefixes.append(running)
    gathered = lax.all_gather(running, "section")
    earlier = (jnp.arange(sections) < section)[:, None, None]
    before = jnp.sum(jnp.where(earlier, gathered, 0.0), axis=0)
    sums = exposures(built, log_spot, before, jnp.stack(prefixes, axis=0), trades)
    totals = summed(sums, "paths")
    return totals / (normal_draws.shape[2] * lax.axis_size("paths"))


def solution(mesh):
    placed = (P("section", None, "paths"), P("section", "paths", None, None)) + (P(),) * 6
    return jax.shard_map(
        shards, mesh=mesh, in_specs=placed, out_specs=P("section", None), check_vma=False
    )
```

time: 77.6 us -> 64.6 us (0.83)
  Pallas kernels: 36.4 us -> 23.5 us
    pallas_call x1, Pallas kernels: 25.5 us -> 16.8 us  [exposures(): pl.pallas_call(exposure_kernel, out_shape=jax.ShapeDtypeStruct((dates, SE...]
    pallas_call x1, Pallas kernels: 10.9 us -> 6.73 us  [tables(): pl.pallas_call(table_kernel, out_shape=(jax.ShapeDtypeStruct(grid_rows, j...]
  transfers between devices with their start and end apart: 6 -> 6, of which waited for: 5 -> 5; matrix products, arithmetic and copies ran while one was open for 3% -> 4% of each run, Pallas kernels for 14% -> 10%
where the time goes in v1:
time: 64.6 us; the launch traced here: 64.3 us
  Pallas kernels  23.5 us (36%)
  starting transfers between devices  11.4 us (18%)
  blocking collectives  10.3 us (16%)
  waiting for transfers between devices  10.2 us (16%)
  other arithmetic  4.16 us (6%)
  local copies, waits for them, and re-layouts  3.77 us (6%)
  matrix products  0.77 us (1%)
    pallas_call x1, Pallas kernels, exposures(): pl.pallas_call(exposure_kernel, out_shape=jax.ShapeDtypeStruct((dates, SE...  16.8 us
    ppermute x6, starting transfers between devices, summed(): lax.ppermute(part, axis, [(i, i ^ distance) for i in range(size)])  11.4 us
    all_gather x1, blocking collectives, shards(): gathered = lax.all_gather(running, 'section')  10.3 us
    ppermute x6, waiting for transfers between devices, summed(): lax.ppermute(part, axis, [(i, i ^ distance) for i in range(size)])  10.2 us
    pallas_call x1, Pallas kernels, tables(): pl.pallas_call(table_kernel, out_shape=(jax.ShapeDtypeStruct(grid_rows, j...  6.73 us
    slice x1, local copies, waits for them, and re-layouts, shards(): normal_draws[date]  1.71 us
    unnamed x6, local copies, waits for them, and re-layouts  1.32 us
  transfers between devices with their start and end apart: 6, of which 5 were waited for; matrix products, arithmetic and copies ran while one was open for 4% of the time, Pallas kernels for 10%

profile of v1, /device:TPU:0, one launch (start us, length us, event | category | flops | bytes accessed | tf_op | source)
XLA Modules:
  0.0 64.3 jit_solution(10925970272196095746)
XLA Ops:
  0.0 0.0 copy-start.2
  0.0 0.7 %copy-done.2 = s32[8]{0:T(128)S(1)} copy-done((s32[8]{0:T(128)S(1)}, s32[8]{0:T(128)}, u32[]{:S(2)}) %copy-start.2) | copy-done | bytes 56
  0.7 0.1 dynamic-slice_compare_fusion
  0.7 0.9 %bitcast_select_fusion = f32[2,60,60]{2,0,1:T(2,128)S(1)} fusion(f32[2,1,60,60]{3,1,2,0:T(1,128)} %param.9, pred[2]{0:T(512)(128)(4,1)S(1)} %dynamic-slice_compare_fusion), kind=kLoop, calls=%fused_computation.7 | loop fusion | flops 7200 | bytes 57602 | tf_op jit(solution)/shard_map/jit(_where)/select_n | solution.py:267
  1.7 0.0 copy-start
  1.7 3.1 %collective-permute-start = (f32[2,60,60]{2,0,1:T(2,128)S(1)}, f32[2,60,60]{2,0,1:T(2,128)S(1)}, u32[]{:S(2)}, u32[]{:S(2)}) collective-permute-start(f32[2,60,60]{2,0,1:T(2,128)S(1)} %bitcast_select_fusion), channel_id=1, source_target_pairs={{0,1},{1,0},{2,3},{3,2},{4,5},{5,4},{6,7},{7,6},{8,9},{9,8},{10,11... | collective-permute-start | bytes 86408 | tf_op jit(solution)/shard_map/ppermute | solution.py:26
  4.7 1.7 %fusion.6 = (f32[1,60,1024]{2,0,1:T(1,128)S(1)}, f32[1,60,1024]{2,0,1:T(1,128)S(1)}) fusion(f32[2,60,1024]{2,0,1:T(2,128)} %param.8), kind=kLoop, calls=%fused_computation.15 | loop fusion | bytes 983040 | tf_op jit(solution)/shard_map/slice | solution.py:273
  6.4 0.5 collective-permute-done
  6.9 0.0 copy-done
  6.9 0.1 fusion.8
  7.0 2.1 %collective-permute-start.1 = (f32[2,60,60]{2,0,1:T(2,128)S(1)}, f32[2,60,60]{2,0,1:T(2,128)S(1)}, u32[]{:S(2)}, u32[]{:S(2)}) collective-permute-start(f32[2,60,60]{2,0,1:T(2,128)S(1)} %fusion.8), channel_id=1, source_target_pairs={{0,2},{1,3},{2,0},{3,1},{4,6},{5,7},{6,4},{7,5},{8,10},{9,11},{10,... | collective-permute-start | bytes 86408 | tf_op jit(solution)/shard_map/ppermute | solution.py:26
  9.2 6.7 %tables.1 = (s32[32,4,128]{2,1,0:T(4,128)}, f32[32,4,128]{2,1,0:T(4,128)}, f32[32,4,128]{2,1,0:T(4,128)}, bf16[512,512]{1,0:T(8,128)(2,1)}, s32[1,512]{1,0:T(1,128)}) custom-call(s32[32,128]{1,0:T(8,128)} %bitcast.32, s32[32,128]{1,0:T(8,128)} %bitcast.33, f32[32,128]{1,0:T(8,128)} %bitcast.34, f32[32,128]{1,0:T(8,128)} %bitcast.35), custom_call_target="tpu_custom_call" | custom-call | flops 2097152000 | bytes 1048576 | tf_op jit(solution)/shard_map/tables/pallas_call | solution.py:121
  15.9 0.0 collective-permute-done.1
  16.0 2.7 %collective-permute-start.2 = (f32[2,60,60]{2,0,1:T(2,128)S(1)}, f32[2,60,60]{2,0,1:T(2,128)S(1)}, u32[]{:S(2)}, u32[]{:S(2)}) collective-permute-start(f32[2,60,60]{2,0,1:T(2,128)S(1)} %add.26), channel_id=1, source_target_pairs={{0,4},{1,5},{2,6},{3,7},{4,0},{5,1},{6,2},{7,3},{8,12},{9,13},{10,... | collective-permute-start | bytes 86408 | tf_op jit(solution)/shard_map/ppermute | solution.py:26
  18.6 0.0 copy-start.1
  18.6 0.7 %copy-done.1 = f32[60]{0:T(128)S(1)} copy-done((f32[60]{0:T(128)S(1)}, f32[60]{0:T(128)}, u32[]{:S(2)}) %copy-start.1) | copy-done | bytes 264
  19.3 0.7 %copy.17.spot_ref = f32[60,1]{1,0:T(8,128)} copy(f32[60,1]{0,1:T(1,128)S(1)} %bitcast.37) | data formatting | bytes 480 | tf_op jit(solution)/shard_map/broadcast_in_dim | solution.py:257
  20.0 1.4 %collective-permute-done.2 = f32[2,60,60]{2,0,1:T(2,128)S(1)} collective-permute-done((f32[2,60,60]{2,0,1:T(2,128)S(1)}, f32[2,60,60]{2,0,1:T(2,128)S(1)}, u32[]{:S(2)}, u32[]{:S(2)}) %collective-permute-start.2) | collective-permute-done | bytes 28832 | tf_op jit(solution)/shard_map/ppermute | solution.py:26
  21.4 0.4 fusion.1
  21.8 0.4 fusion
  22.2 10.3 %all-gather.1 = f32[4,60,1024]{2,1,0:T(8,128)S(1)} all-gather(f32[1,60,1024]{2,1,0:T(8,128)S(1)} %fusion), channel_id=2, replica_groups=mesh['section'=4,'paths'=8] {'section'}, dimensions={0}, use_global_device_ids=true | all-gather | bytes 1228800 | tf_op jit(solution)/shard_map/all_gather | solution.py:279
  32.6 0.8 %pad_maximum_fusion.own_ref = f32[2,60,1024]{2,1,0:T(8,128)} fusion(f32[1,60,1024]{2,1,0:T(8,128)S(1)} %fusion, f32[1,60,1024]{2,1,0:T(8,128)S(1)} %bitcast.28), kind=kLoop, calls=%fused_computation.3 | loop fusion | flops 122880 | bytes 983040 | tf_op jit(solution)/shard_map/stack | solution.py:282
  33.4 0.9 %select_reduce_fusion.carry_ref = f32[60,1024]{1,0:T(8,128)} fusion(f32[4,60,1024]{2,1,0:T(8,128)S(1)} %all-gather.1, pred[4]{0:T(512)(128)(4,1)S(1)} %iota_compare_fusion), kind=kLoop, calls=%fused_computation.2 | loop fusion | flops 430080 | bytes 1228804 | tf_op jit(solution)/shard_map/reduce_sum | solution.py:281
  34.3 16.8 %exposures.1 = f32[2,512]{1,0:T(2,128)} custom-call(s32[512]{0:T(512)} %bitcast.36, s32[16384]{0:T(1024)} %bitcast.29, f32[16384]{0:T(1024)} %bitcast.30, f32[16384]{0:T(1024)} %bitcast.31, bf16[512,512]{1,0:T(8,128)(2,1)} %get-tuple-element.14.place_ref, f32[60,1]{1,0:T(8,128)} %copy.17.spot_ref, f32[60,1024]{1,0:T(8,128)} %select_reduce_fusion.carry_ref, ...), custom_call_target="tpu_custom_call" | custom-call | tf_op jit(solution)/shard_map/exposures/pallas_call | solution.py:241
  51.0 1.5 %collective-permute-start.3 = (f32[2,512]{1,0:T(2,128)}, f32[2,512]{1,0:T(2,128)S(1)}, u32[]{:S(2)}, u32[]{:S(2)}) collective-permute-start(f32[2,512]{1,0:T(2,128)} %exposures.1), channel_id=1, source_target_pairs={{0,1},{1,0},{2,3},{3,2},{4,5},{5,4},{6,7},{7,6},{8,9},{9,8},{10,11... | collective-permute-start | bytes 12296 | tf_op jit(solution)/shard_map/ppermute | solution.py:26
  52.6 2.3 %collective-permute-done.3 = f32[2,512]{1,0:T(2,128)S(1)} collective-permute-done((f32[2,512]{1,0:T(2,128)}, f32[2,512]{1,0:T(2,128)S(1)}, u32[]{:S(2)}, u32[]{:S(2)}) %collective-permute-start.3) | collective-permute-done | bytes 4128 | tf_op jit(solution)/shard_map/ppermute | solution.py:26
  54.9 0.7 %add.29 = f32[2,512]{1,0:T(2,128)S(1)} add(f32[2,512]{1,0:T(2,128)} %exposures.1, f32[2,512]{1,0:T(2,128)S(1)} %collective-permute-done.3) | non-fusion elementwise | flops 1024 | bytes 12288 | tf_op jit(solution)/shard_map/add | solution.py:26
  55.6 0.0 collective-permute-start.4
  55.6 3.6 %collective-permute-done.4 = f32[2,512]{1,0:T(2,128)S(1)} collective-permute-done((f32[2,512]{1,0:T(2,128)S(1)}, f32[2,512]{1,0:T(2,128)S(1)}, u32[]{:S(2)}, u32[]{:S(2)}) %collective-permute-start.4) | collective-permute-done | bytes 4128 | tf_op jit(solution)/shard_map/ppermute | solution.py:26
  59.2 2.0 %collective-permute-start.5 = (f32[2,512]{1,0:T(2,128)S(1)}, f32[2,512]{1,0:T(2,128)S(1)}, u32[]{:S(2)}, u32[]{:S(2)}) collective-permute-start(f32[2,512]{1,0:T(2,128)S(1)} %add.30), channel_id=1, source_target_pairs={{0,4},{1,5},{2,6},{3,7},{4,0},{5,1},{6,2},{7,3},{8,12},{9,13},{10,... | collective-permute-start | bytes 12296 | tf_op jit(solution)/shard_map/ppermute | solution.py:26
  61.2 2.5 %collective-permute-done.5 = f32[2,512]{1,0:T(2,128)S(1)} collective-permute-done((f32[2,512]{1,0:T(2,128)S(1)}, f32[2,512]{1,0:T(2,128)S(1)}, u32[]{:S(2)}, u32[]{:S(2)}) %collective-permute-start.5) | collective-permute-done | bytes 4128 | tf_op jit(solution)/shard_map/ppermute | solution.py:26
  63.7 0.6 add_multiply_fusion
  (5 shorter events, 0.1 us)
Async XLA Ops:
  0.0 0.7 %copy-start.2 = (s32[8]{0:T(128)S(1)}, s32[8]{0:T(128)}, u32[]{:S(2)}) copy-start(s32[8]{0:T(128)} %param.11) | copy-start | bytes 100
  1.7 5.3 %copy-start = (f32[2,1,60,60]{3,1,2,0:T(1,128)S(1)}, f32[2,1,60,60]{3,1,2,0:T(1,128)}, u32[]{:S(2)}) copy-start(f32[2,1,60,60]{3,1,2,0:T(1,128)} %param.9) | copy-start | bytes 86404
  1.7 5.3 %collective-permute-start = (f32[2,60,60]{2,0,1:T(2,128)S(1)}, f32[2,60,60]{2,0,1:T(2,128)S(1)}, u32[]{:S(2)}, u32[]{:S(2)}) collective-permute-start(f32[2,60,60]{2,0,1:T(2,128)S(1)} %bitcast_select_fusion), channel_id=1, source_target_pairs={{0,1},{1,0},{2,3},{3,2},{4,5},{5,4},{6,7},{7,6},{8,9},{9,8},{10,11... | collective-permute-start | bytes 86408 | tf_op jit(solution)/shard_map/ppermute | solution.py:26
  7.0 8.9 %collective-permute-start.1 = (f32[2,60,60]{2,0,1:T(2,128)S(1)}, f32[2,60,60]{2,0,1:T(2,128)S(1)}, u32[]{:S(2)}, u32[]{:S(2)}) collective-permute-start(f32[2,60,60]{2,0,1:T(2,128)S(1)} %fusion.8), channel_id=1, source_target_pairs={{0,2},{1,3},{2,0},{3,1},{4,6},{5,7},{6,4},{7,5},{8,10},{9,11},{10,... | collective-permute-start | bytes 86408 | tf_op jit(solution)/shard_map/ppermute | solution.py:26
  16.0 5.4 %collective-permute-start.2 = (f32[2,60,60]{2,0,1:T(2,128)S(1)}, f32[2,60,60]{2,0,1:T(2,128)S(1)}, u32[]{:S(2)}, u32[]{:S(2)}) collective-permute-start(f32[2,60,60]{2,0,1:T(2,128)S(1)} %add.26), channel_id=1, source_target_pairs={{0,4},{1,5},{2,6},{3,7},{4,0},{5,1},{6,2},{7,3},{8,12},{9,13},{10,... | collective-permute-start | bytes 86408 | tf_op jit(solution)/shard_map/ppermute | solution.py:26
  18.6 0.7 %copy-start.1 = (f32[60]{0:T(128)S(1)}, f32[60]{0:T(128)}, u32[]{:S(2)}) copy-start(f32[60]{0:T(128)} %param.10) | copy-start | bytes 724
  51.0 3.8 %collective-permute-start.3 = (f32[2,512]{1,0:T(2,128)}, f32[2,512]{1,0:T(2,128)S(1)}, u32[]{:S(2)}, u32[]{:S(2)}) collective-permute-start(f32[2,512]{1,0:T(2,128)} %exposures.1), channel_id=1, source_target_pairs={{0,1},{1,0},{2,3},{3,2},{4,5},{5,4},{6,7},{7,6},{8,9},{9,8},{10,11... | collective-permute-start | bytes 12296 | tf_op jit(solution)/shard_map/ppermute | solution.py:26
  55.6 3.6 %collective-permute-start.4 = (f32[2,512]{1,0:T(2,128)S(1)}, f32[2,512]{1,0:T(2,128)S(1)}, u32[]{:S(2)}, u32[]{:S(2)}) collective-permute-start(f32[2,512]{1,0:T(2,128)S(1)} %add.29), channel_id=1, source_target_pairs={{0,2},{1,3},{2,0},{3,1},{4,6},{5,7},{6,4},{7,5},{8,10},{9,11},{10,... | collective-permute-start | bytes 12296 | tf_op jit(solution)/shard_map/ppermute | solution.py:26
  59.2 4.5 %collective-permute-start.5 = (f32[2,512]{1,0:T(2,128)S(1)}, f32[2,512]{1,0:T(2,128)S(1)}, u32[]{:S(2)}, u32[]{:S(2)}) collective-permute-start(f32[2,512]{1,0:T(2,128)S(1)} %add.30), channel_id=1, source_target_pairs={{0,4},{1,5},{2,6},{3,7},{4,0},{5,1},{6,2},{7,3},{8,12},{9,13},{10,... | collective-permute-start | bytes 12296 | tf_op jit(solution)/shard_map/ppermute | solution.py:26

commit v2 on v1

--- a/solution.py
+++ b/solution.py
@@ -13,8 +13,10 @@
 BLOCKS = SETS // LANES
 CHUNK = 2 * LANES
 ROWS = 32
+PAIRS = ROWS // 2
+SHIFT = 16
 GROUP = 16
-UNROLL = 2
+PARTS = 4
 
 
 def summed(part, axis):
@@ -43,8 +45,13 @@
     return lax.broadcasted_iota(jnp.int32, shape, dim)
 
 
+def moves(place):
+    hot = iota((SETS, SETS), 0).astype(jnp.float32) == place
+    return hot.astype(jnp.float32).astype(jnp.bfloat16)
+
+
 def table_kernel(
-    factor_ref, set_ref, notional_ref, level_ref,
+    step, factor_ref, set_ref, notional_ref, level_ref,
     index_ref, strike_ref, weight_ref, place_ref, count_ref,
     before_ref, base_ref, table_ref,
 ):
@@ -53,12 +60,13 @@
     base_ref[...] = jnp.zeros_like(base_ref)
     table_ref[...] = jnp.zeros_like(table_ref)
     set_ids = iota((SETS, LANES), 0)
-    row_ids = iota((ROWS, LANES), 0).astype(jnp.float32)
-
-    def chunk(step, carry):
+    rows_at = iota((ROWS, LANES), 0)
+    row_ids = jnp.where(rows_at < PAIRS, 2 * rows_at, 2 * (rows_at - PAIRS) + 1).astype(jnp.float32)
+
+    def chunk(turn, carry):
         masks, rows = [], []
         for half in range(2):
-            masks.append(set_ids == set_ref[pl.ds(2 * step + half, 1), :])
+            masks.append(set_ids == set_ref[pl.ds(2 * turn + half, 1), :])
         hot = jnp.concatenate([m.astype(jnp.float32).astype(jnp.bfloat16) for m in masks], axis=1)
         earlier = jnp.dot(hot, before_ref[...], preferred_element_type=jnp.float32)
         base = base_ref[...]
@@ -68,7 +76,7 @@
                 axis=0, keepdims=True,
             )
             here = row_ids == rank
-            own = pl.ds(2 * step + half, 1)
+            own = pl.ds(2 * turn + half, 1)
             values = (
                 (factor_ref[own, :].astype(jnp.float32),)
                 + pieces(level_ref[own, :])
@@ -96,35 +104,36 @@
         ahead = (base > own) | ((base == own) & (set_ids < mine))
         places.append(jnp.sum(jnp.where(ahead, 1.0, 0.0), axis=0, keepdims=True))
     place = jnp.concatenate(places, axis=1)
-    moved = (iota((SETS, SETS), 0).astype(jnp.float32) == place).astype(jnp.float32)
-    moved = moved.astype(jnp.bfloat16)
-    place_ref[...] = moved
+    moved = moves(place)
+    place_ref[...] = place
     table = dot_last(table[: 7 * ROWS, :].astype(jnp.bfloat16), moved)
     index = table[:ROWS, :].astype(jnp.int32)
+    index = (index[:PAIRS] + (index[PAIRS:] << SHIFT)) * step
     strike = table[ROWS : 2 * ROWS] + (table[2 * ROWS : 3 * ROWS] + table[3 * ROWS : 4 * ROWS])
     weight = table[4 * ROWS : 5 * ROWS] + (table[5 * ROWS : 6 * ROWS] + table[6 * ROWS : 7 * ROWS])
     for block in range(BLOCKS):
         own = slice(block * LANES, (block + 1) * LANES)
         index_ref[:, block, :] = index[:, own]
-        strike_ref[:, block, :] = strike[:, own]
-        weight_ref[:, block, :] = weight[:, own]
+        for half in range(2):
+            at = slice(half * PAIRS, (half + 1) * PAIRS)
+            strike_ref[:, half * BLOCKS + block, :] = strike[at, own]
+            weight_ref[:, half * BLOCKS + block, :] = weight[at, own]
     exact = jnp.concatenate([(counts - LOW * jnp.floor(counts / LOW)), jnp.floor(counts / LOW)] + [jnp.zeros((14, SETS), jnp.float32)], axis=0)
     ordered = dot_last(exact.astype(jnp.bfloat16), moved)
     count_ref[...] = (ordered[:1] + LOW * ordered[1:2]).astype(jnp.int32)
 
 
-def tables(trade_factor, trade_set, notional, strike):
+def tables(step, trade_factor, trade_set, notional, strike):
     lines = trade_factor.shape[0] // LANES
     packed = [a.reshape(lines, LANES) for a in (trade_factor, trade_set, notional, strike)]
     vmem = pl.BlockSpec(memory_space=pltpu.VMEM)
-    grid_rows = (ROWS, BLOCKS, LANES)
     return pl.pallas_call(
-        table_kernel,
+        functools.partial(table_kernel, step),
         out_shape=(
-            jax.ShapeDtypeStruct(grid_rows, jnp.int32),
-            jax.ShapeDtypeStruct(grid_rows, jnp.float32),
-            jax.ShapeDtypeStruct(grid_rows, jnp.float32),
-            jax.ShapeDtypeStruct((SETS, SETS), jnp.bfloat16),
+            jax.ShapeDtypeStruct((PAIRS, BLOCKS, LANES), jnp.int32),
+            jax.ShapeDtypeStruct((PAIRS, 2 * BLOCKS, LANES), jnp.float32),
+            jax.ShapeDtypeStruct((PAIRS, 2 * BLOCKS, LANES), jnp.float32),
+            jax.ShapeDtypeStruct((1, SETS), jnp.float32),
             jax.ShapeDtypeStruct((1, SETS), jnp.int32),
         ),
         in_specs=[vmem] * 4,
@@ -137,6 +146,7 @@
         cost_estimate=pl.CostEstimate(
             flops=2 * trade_factor.shape[0] * SETS * 500, transcendentals=0, bytes_accessed=1 << 20
         ),
+        compiler_params=pltpu.CompilerParams(vmem_limit_bytes=8 << 20),
         name="tables",
     )(*packed)
 
@@ -153,40 +163,69 @@
 
 
 def exposure_kernel(
-    count_ref, index_ref, strike_ref, weight_ref, place_ref, spot_ref, carry_ref, own_ref,
+    count_ref, index_hbm, level_hbm, weight_hbm, place_ref, carry_ref, first_ref, second_ref,
     factor_hbm, set_hbm, notional_hbm, strike_hbm,
     out_ref,
-    level_ref, price_ref, sum_ref, net_ref, factor_s, set_s, notional_s, strike_s,
+    index_ref, limit_ref, weight_ref, copied, level_ref, price_ref, sum_ref, net_ref, factor_s, set_s, notional_s, strike_s,
 ):
-    dates, factors, paths = own_ref.shape
+    own_refs = (first_ref, second_ref)
+    dates, (factors, paths) = len(own_refs), first_ref.shape
     tiles = paths // LANES
-    carried = carry_ref[...] + spot_ref[...]
+    largest = count_ref[0]
+    fits = largest <= ROWS
+    copies = []
+    for part in range(PARTS):
+        each = PAIRS // PARTS
+        wanted = fits & ((largest > 2 * each * part) | (part == 0))
+        both = []
+        for source, target, row in ((index_hbm, index_ref, SETS), (level_hbm, limit_ref, 2 * SETS), (weight_hbm, weight_ref, 2 * SETS)):
+            at = pl.ds(part * each * row, each * row)
+            both.append(pltpu.make_async_copy(source.at[at], target.at[at], copied.at[part, len(both)]))
+        copies.append((wanted, both))
+
+        @pl.when(wanted)
+        def _(both=both):
+            for copy in both:
+                copy.start()
+
+    stacked_ref = price_ref.reshape(factors, dates, tiles, LANES)
+    carried = carry_ref[...]
     for date in range(dates):
-        level = jnp.exp(carried + own_ref[date])
+        level = jnp.exp(carried + own_refs[date][...])
         level_ref[date] = level
-        price_ref[:, date] = level.reshape(factors, tiles, LANES)
-    largest = count_ref[0]
-
-    @pl.when(largest <= ROWS)
+        stacked_ref[:, date] = level.reshape(factors, tiles, LANES)
+
+    @pl.when(fits)
     def _():
         def group(step, carry):
-            first = step * GROUP
+            first = (SETS // GROUP - 1 - step) * GROUP
+            count = count_ref[first]
+            smaller = jnp.where(step == 0, -1, count_ref[jnp.minimum(first + GROUP, SETS - 1)])
+            for part, (_, both) in enumerate(copies):
+                needed = 2 * (PAIRS // PARTS) * part if part else -1
+
+                @pl.when((count > needed) & (smaller <= needed))
+                def _(both=both):
+                    for copy in both:
+                        copy.wait()
 
             def rows(r, nets):
                 nets = [list(n) for n in nets]
-                base = r * (UNROLL * SETS) + first
-                for u in range(UNROLL):
+                packs = index_ref.at[pl.ds(r * SETS + first, GROUP)]
+                for u in range(2):
+                    at = pl.ds(r * (2 * SETS) + u * SETS + first, GROUP)
+                    strikes, weights = limit_ref.at[at], weight_ref.at[at]
                     for j in range(GROUP):
-                        slot = base + u * SETS + j
-                        index, strike, weight = index_ref[slot], strike_ref[slot], weight_ref[slot]
+                        index = packs[j] >> SHIFT if u else packs[j] & ((1 << SHIFT) - 1)
+                        strike, weight = strikes[j], weights[j]
                         for date in range(dates):
-                            price = price_ref[index, date]
+                            price = price_ref[pl.ds(pl.multiple_of(index + date * tiles, 8), tiles), :]
                             nets[date][j] += weight * jnp.maximum(price - strike, 0.0)
                 return tuple(tuple(n) for n in nets)
 
             zero = jnp.zeros((tiles, LANES), jnp.float32)
             nets = lax.fori_loop(
-                0, (count_ref[first] + UNROLL - 1) // UNROLL, rows, ((zero,) * GROUP,) * dates
+                0, (count + 1) // 2, rows, ((zero,) * GROUP,) * dates
             )
             for date in range(dates):
                 for part in range(GROUP // 8):
@@ -201,8 +240,8 @@
         for date in range(dates):
             lines.append(sum(dot_last(ones, p.astype(jnp.bfloat16)) for p in pieces(sum_ref[date]))[:1])
         total = jnp.concatenate(lines + [jnp.zeros((16 - dates, SETS), jnp.float32)], axis=0)
-        place = place_ref[...]
-        parts = [jnp.dot(p.astype(jnp.bfloat16), place, preferred_element_type=jnp.float32) for p in pieces(total)]
+        moved = moves(place_ref[...])
+        parts = [jnp.dot(p.astype(jnp.bfloat16), moved, preferred_element_type=jnp.float32) for p in pieces(total)]
         out_ref[...] = (parts[0] + (parts[1] + parts[2]))[:dates]
 
     @pl.when(largest > ROWS)
@@ -233,19 +272,23 @@
         lax.fori_loop(0, dates, one_date, 0)
 
 
-def exposures(built, log_spot, before, own, trades):
-    index, strike, weight, place, count = built
-    dates, factors, paths = own.shape
+def exposures(built, before, first, second, trades):
+    index, level, weight, place, count = built
+    dates, (factors, paths) = 2, first.shape
     vmem, hbm = pl.BlockSpec(memory_space=pltpu.VMEM), pl.BlockSpec(memory_space=pl.ANY)
     number = trades[0].shape
     return pl.pallas_call(
         exposure_kernel,
         out_shape=jax.ShapeDtypeStruct((dates, SETS), jnp.float32),
-        in_specs=[pl.BlockSpec(memory_space=pltpu.SMEM)] * 4 + [vmem] * 4 + [hbm] * 4,
+        in_specs=[pl.BlockSpec(memory_space=pltpu.SMEM)] + [hbm] * 3 + [vmem] * 4 + [hbm] * 4,
         out_specs=vmem,
         scratch_shapes=[
+            pltpu.SMEM((PAIRS * SETS,), jnp.int32),
+            pltpu.SMEM((PAIRS * 2 * SETS,), jnp.float32),
+            pltpu.SMEM((PAIRS * 2 * SETS,), jnp.float32),
+            pltpu.SemaphoreType.DMA((PARTS, 3)),
             pltpu.VMEM((dates, factors, paths), jnp.float32),
-            pltpu.VMEM((factors, dates, paths // LANES, LANES), jnp.float32),
+            pltpu.VMEM((factors * dates * (paths // LANES), LANES), jnp.float32),
             pltpu.VMEM((dates, SETS, LANES), jnp.float32),
             pltpu.VMEM((SETS, paths), jnp.float32),
             pltpu.SMEM(number, jnp.int32),
@@ -253,35 +296,66 @@
             pltpu.SMEM(number, jnp.float32),
             pltpu.SMEM(number, jnp.float32),
         ],
+        compiler_params=pltpu.CompilerParams(vmem_limit_bytes=12 << 20),
         name="exposures",
-    )(count.reshape(SETS), index.reshape(-1), strike.reshape(-1), weight.reshape(-1), place, log_spot[:, None], before, own, *trades)
+    )(count.reshape(SETS), index.reshape(-1), level.reshape(-1), weight.reshape(-1), place, before, first, second, *trades)
+
+
+def carried_in(total, fill):
+    sections, section = lax.axis_size("section"), lax.axis_index("section")
+    before = jnp.zeros_like(total)
+    middle = total.shape[1] // 2
+    odd = (section & 1) == 1
+    distance, filled = 1, None
+    while distance < sections:
+        last = 2 * distance == sections
+        pairs = [(i, i ^ distance) for i in range(sections) if not (last and i & distance)]
+        if distance == 1:
+            got = lax.ppermute(total, "section", pairs)
+        else:
+            half = jnp.where(odd, total[:, middle:], total[:, :middle])
+            if filled is None:
+                half, filled = fill(half)
+            own = lax.ppermute(half, "section", pairs)
+            own, filled = lax.optimization_barrier((own, filled))
+            other = lax.ppermute(own, "section", [(i, i ^ 1) for i in range(sections)])
+            got = jnp.concatenate([jnp.where(odd, other, own), jnp.where(odd, own, other)], axis=1)
+        before = before + jnp.where((section & distance) != 0, got, 0.0)
+        if not last:
+            total = total + got
+        distance *= 2
+    return before, fill(total)[1] if filled is None else filled
 
 
 def shards(normal_draws, cholesky, log_spot, owner, trade_factor, trade_set, notional, strike):
-    local_dates = normal_draws.shape[0]
-    section, sections = lax.axis_index("section"), lax.axis_size("section")
+    dates, factors, paths = normal_draws.shape
+    half = LANES // 2
+    section = lax.axis_index("section")
     trades = (trade_factor, trade_set, notional, strike)
-    built = tables(*trades)
-    owners_here = lax.dynamic_slice_in_dim(owner, section * local_dates, local_dates)
-    mine = (owners_here == lax.axis_index("paths"))[:, None, None]
-    blocks = summed(jnp.where(mine, cholesky[:, 0], 0.0), "paths")
-    running = jnp.zeros(normal_draws.shape[1:], jnp.float32)
-    prefixes = []
-    for date in range(local_dates):
-        increment = jnp.dot(
-            blocks[date],
-            normal_draws[date],
+    owners_here = lax.dynamic_slice_in_dim(owner, section * dates, dates)
+    mine = owners_here == lax.axis_index("paths")
+    spare = ((0, 0), (0, half - factors))
+    packed = [jnp.pad(jnp.where(mine[d], cholesky[d, 0], 0.0), spare) for d in range(dates)]
+    blocks = summed(jnp.concatenate(packed, axis=1), "paths")
+    draws = jnp.pad(normal_draws, ((0, 0), (0, half - factors), (0, 0))).reshape(dates * half, paths)
+    first, second = (
+        jnp.dot(
+            blocks[:, : (date + 1) * half],
+            draws[: (date + 1) * half],
             precision=lax.Precision.HIGHEST,
             preferred_element_type=jnp.float32,
         )
-        running = running + increment
-        prefixes.append(running)
-    gathered = lax.all_gather(running, "section")
-    earlier = (jnp.arange(sections) < section)[:, None, None]
-    before = jnp.sum(jnp.where(earlier, gathered, 0.0), axis=0)
-    sums = exposures(built, log_spot, before, jnp.stack(prefixes, axis=0), trades)
+        for date in range(dates)
+    )
+
+    def fill(ready, first=first):
+        ready, own, tied = lax.optimization_barrier((ready, first, trades))
+        return ready, (own, tables(dates * paths // LANES, *tied))
+
+    before, (first, built) = carried_in(second, fill)
+    sums = exposures(built, before + log_spot[:, None], first, second, trades)
     totals = summed(sums, "paths")
-    return totals / (normal_draws.shape[2] * lax.axis_size("paths"))
+    return totals / (paths * lax.axis_size("paths"))
 
 
 def solution(mesh):

time: 64.6 us -> 57 us (0.88)
  blocking collectives: 10.3 us -> 0 us
  starting transfers between devices: 11.4 us -> 17.8 us
  Pallas kernels: 23.5 us -> 18.6 us
  waiting for transfers between devices: 10.2 us -> 14 us
  local copies, waits for them, and re-layouts: 3.77 us -> 1.54 us
    all_gather x1 -> x0, blocking collectives: 10.3 us -> none  [shards(): gathered = lax.all_gather(running, 'section')]
    ppermute x0 -> x3, starting transfers between devices: none -> 3.88 us  [the longest x1 3.74 us: carried_in(): own = lax.ppermute(half, 'section', pairs)]
    pallas_call x1, Pallas kernels: 16.8 us -> 13.5 us  [exposures(): pl.pallas_call(exposure_kernel, out_shape=jax.ShapeDtypeStruct((dates, SE...]
    ppermute x0 -> x3, waiting for transfers between devices: none -> 2.48 us  [the longest x1 1.33 us: carried_in(): other = lax.ppermute(own, 'section', [(i, i ^ 1) for i in range(sections)])]
    ppermute x6, starting transfers between devices: 11.4 us -> 13.9 us  [summed(): lax.ppermute(part, axis, [(i, i ^ distance) for i in range(size)])]
    pallas_call x1, Pallas kernels: 6.73 us -> 5.09 us  [tables(): pl.pallas_call(functools.partial(table_kernel, step), out_shape=(jax.Shap...]
    slice x0 -> x1, other arithmetic: none -> 1.49 us  [shards(): cholesky[d, 0]]
    ppermute x6, waiting for transfers between devices: 10.2 us -> 11.5 us  [summed(): lax.ppermute(part, axis, [(i, i ^ distance) for i in range(size)])]
  transfers between devices with their start and end apart: 6 -> 9, of which waited for: 5 -> 8; matrix products, arithmetic and copies ran while one was open for 4% -> 1% of each run, Pallas kernels for 10% -> 9%
where the time goes in v2:
time: 57 us; the launch traced here: 56.7 us
  Pallas kernels  18.6 us (33%)
  starting transfers between devices  17.8 us (31%)
  waiting for transfers between devices  14 us (25%)
  other arithmetic  3.86 us (7%)
  local copies, waits for them, and re-layouts  1.54 us (3%)
  matrix products  0.79 us (1%)
    ppermute x6, starting transfers between devices, summed(): lax.ppermute(part, axis, [(i, i ^ distance) for i in range(size)])  13.9 us
    pallas_call x1, Pallas kernels, exposures(): pl.pallas_call(exposure_kernel, out_shape=jax.ShapeDtypeStruct((dates, SE...  13.5 us
    ppermute x6, waiting for transfers between devices, summed(): lax.ppermute(part, axis, [(i, i ^ distance) for i in range(size)])  11.5 us
    pallas_call x1, Pallas kernels, tables(): pl.pallas_call(functools.partial(table_kernel, step), out_shape=(jax.Shap...  5.09 us
    ppermute x1, starting transfers between devices, carried_in(): own = lax.ppermute(half, 'section', pairs)  3.74 us
    slice x1, other arithmetic, shards(): cholesky[d, 0]  1.49 us
    ppermute x1, waiting for transfers between devices, carried_in(): other = lax.ppermute(own, 'section', [(i, i ^ 1) for i in range(sections)])  1.33 us
    ppermute x1, waiting for transfers between devices, carried_in(): got = lax.ppermute(total, 'section', pairs)  1.15 us
  transfers between devices with their start and end apart: 9, of which 8 were waited for; matrix products, arithmetic and copies ran while one was open for 1% of the time, Pallas kernels for 9%

profile of v2, /device:TPU:0, one launch (start us, length us, event | category | flops | bytes accessed | tf_op | source)
XLA Modules:
  0.0 56.7 jit_solution(12739781009723447390)
XLA Ops:
  0.0 0.0 copy-start.4
  0.0 0.8 %dynamic-slice_compare_fusion = pred[2]{0:T(512)(128)(4,1)S(1)} fusion(s32[8]{0:T(128)} %param.11, s32[]{:T(128)S(6)} %select_n.54, s32[]{:T(128)S(6)} %axis_index.29), kind=kLoop, calls=%fused_computation.18 | loop fusion | flops 2 | bytes 18 | tf_op jit(solution)/shard_map/eq | solution.py:336
  0.8 0.7 %fusion.9 = (pred[1]{0:T(512)(128)(4,1)}, pred[1]{0:T(512)(128)(4,1)}) fusion(pred[2]{0:T(512)(128)(4,1)S(1)} %dynamic-slice_compare_fusion), kind=kLoop, calls=%fused_computation.21 | loop fusion | bytes 4 | tf_op jit(solution)/shard_map/slice | solution.py:338
  1.5 1.5 %fusion.8 = (f32[1,1,60,60]{3,1,2,0:T(1,128)S(1)}, f32[1,1,60,60]{3,1,2,0:T(1,128)S(1)}) fusion(f32[2,1,60,60]{3,1,2,0:T(1,128)} %param.9, pred[]{:T(512)} %bitcast.2), kind=kLoop, calls=%fused_computation.20 | loop fusion | flops 3600 | bytes 57601 | tf_op jit(solution)/shard_map/slice | solution.py:338
  2.9 0.7 %fusion.6 = (f32[60,60]{1,0:T(8,128)S(1)}, f32[60,60]{1,0:T(8,128)S(1)}) fusion(f32[1,1,60,60]{3,1,2,0:T(1,128)S(1)} %get-tuple-element.43, pred[]{:T(512)} %bitcast, f32[1,1,60,60]{3,1,2,0:T(1,128)S(1)} %get-tuple-element.44), kind=kLoop, calls=%fused_computation.15 | loop fusion | flops 3600 | bytes 57601 | tf_op jit(solution)/shard_map/jit(_where)/select_n | solution.py:338
  3.6 0.1 select_maximum_fusion
  3.7 3.0 %collective-permute-start = (f32[60,128]{1,0:T(8,128)S(1)}, f32[60,128]{1,0:T(8,128)S(1)}, u32[]{:S(2)}, u32[]{:S(2)}) collective-permute-start(f32[60,128]{1,0:T(8,128)S(1)} %select_maximum_fusion), channel_id=1, source_target_pairs={{0,1},{1,0},{2,3},{3,2},{4,5},{5,4},{6,7},{7,6},{8,9},{9,8},{10,11... | collective-permute-start | bytes 92168 | tf_op jit(solution)/shard_map/ppermute | solution.py:28
  6.7 1.9 %collective-permute-done = f32[60,128]{1,0:T(8,128)S(1)} collective-permute-done((f32[60,128]{1,0:T(8,128)S(1)}, f32[60,128]{1,0:T(8,128)S(1)}, u32[]{:S(2)}, u32[]{:S(2)}) %collective-permute-start) | collective-permute-done | bytes 30752 | tf_op jit(solution)/shard_map/ppermute | solution.py:28
  8.6 0.1 fusion.14
  8.7 2.1 %collective-permute-start.1 = (f32[60,128]{1,0:T(8,128)S(1)}, f32[60,128]{1,0:T(8,128)S(1)}, u32[]{:S(2)}, u32[]{:S(2)}) collective-permute-start(f32[60,128]{1,0:T(8,128)S(1)} %fusion.14), channel_id=1, source_target_pairs={{0,2},{1,3},{2,0},{3,1},{4,6},{5,7},{6,4},{7,5},{8,10},{9,11},{10,... | collective-permute-start | bytes 92168 | tf_op jit(solution)/shard_map/ppermute | solution.py:28
  10.8 1.9 %collective-permute-done.1 = f32[60,128]{1,0:T(8,128)S(1)} collective-permute-done((f32[60,128]{1,0:T(8,128)S(1)}, f32[60,128]{1,0:T(8,128)S(1)}, u32[]{:S(2)}, u32[]{:S(2)}) %collective-permute-start.1) | collective-permute-done | bytes 30752 | tf_op jit(solution)/shard_map/ppermute | solution.py:28
  12.7 3.0 %collective-permute-start.2 = (f32[60,128]{1,0:T(8,128)S(1)}, f32[60,128]{1,0:T(8,128)S(1)}, u32[]{:S(2)}, u32[]{:S(2)}) collective-permute-start(f32[60,128]{1,0:T(8,128)S(1)} %add.43), channel_id=1, source_target_pairs={{0,4},{1,5},{2,6},{3,7},{4,0},{5,1},{6,2},{7,3},{8,12},{9,13},{10,... | collective-permute-start | bytes 92168 | tf_op jit(solution)/shard_map/ppermute | solution.py:28
  15.7 0.0 copy-done.4
  15.7 0.2 copy.13
  15.9 1.7 %collective-permute-done.2 = f32[60,128]{1,0:T(8,128)S(1)} collective-permute-done((f32[60,128]{1,0:T(8,128)S(1)}, f32[60,128]{1,0:T(8,128)S(1)}, u32[]{:S(2)}, u32[]{:S(2)}) %collective-permute-start.2) | collective-permute-done | bytes 30752 | tf_op jit(solution)/shard_map/ppermute | solution.py:28
  17.6 0.4 fusion.11.second_ref
  18.0 0.1 collective-permute-start.3
  18.1 0.4 fusion.2.first_ref
  18.5 1.2 %collective-permute-done.3 = f32[60,1024]{1,0:T(8,128)S(1)} collective-permute-done((f32[60,1024]{1,0:T(8,128)S(1)}, f32[60,1024]{1,0:T(8,128)S(1)}, u32[]{:S(2)}, u32[]{:S(2)}) %collective-permute-start.3) | collective-permute-done | bytes 245792 | tf_op jit(solution)/shard_map/ppermute | solution.py:314
  19.7 0.0 copy-start
  19.7 0.0 copy-start.1
  19.7 0.0 copy-start.2
  19.7 0.0 copy-start.3
  19.7 3.7 %collective-permute-start.4 = (f32[60,512]{1,0:T(8,128)S(1)}, f32[60,512]{1,0:T(8,128)S(1)}, u32[]{:S(2)}, u32[]{:S(2)}) collective-permute-start(f32[60,512]{1,0:T(8,128)S(1)} %slice_select_fusion), channel_id=1, source_target_pairs={{0,16},{8,24},{1,17},{9,25},{2,18},{10,26},{3,19},{11,27},{4,20},{... | collective-permute-start | bytes 368648 | tf_op jit(solution)/shard_map/ppermute | solution.py:319
  23.5 0.0 copy-done
  23.5 0.0 copy-done.1
  23.5 0.0 copy-done.2
  23.5 0.0 copy-done.3
  23.5 5.1 %tables.1 = (s32[16,4,128]{2,1,0:T(4,128)S(1)}, f32[16,8,128]{2,1,0:T(8,128)S(1)}, f32[16,8,128]{2,1,0:T(8,128)S(1)}, f32[1,512]{1,0:T(1,128)S(1)}, s32[1,512]{1,0:T(1,128)S(1)}) custom-call(s32[32,128]{1,0:T(8,128)S(1)} %bitcast.23, s32[32,128]{1,0:T(8,128)S(1)} %bitcast.24, f32[32,128]{1,0:T(8,128)S(1)} %bitcast.25, f32[32,128]{1,0:T(8,128)S(1)} %bitcast.26), custom_call_target="tpu_custom_call" | custom-call | flops 2097152000 | bytes 1048576 | tf_op jit(solution)/shard_map/tables/pallas_call | solution.py:130
  28.6 0.0 collective-permute-done.4
  28.6 0.1 collective-permute-start.5
  28.7 1.3 %collective-permute-done.5 = f32[60,512]{1,0:T(8,128)S(1)} collective-permute-done((f32[60,512]{1,0:T(8,128)S(1)}, f32[60,512]{1,0:T(8,128)S(1)}, u32[]{:S(2)}, u32[]{:S(2)}) %collective-permute-start.5) | collective-permute-done | bytes 122912 | tf_op jit(solution)/shard_map/ppermute | solution.py:321
  30.1 0.0 copy-start.5
  30.1 0.6 %copy-done.5 = f32[60]{0:T(128)S(1)} copy-done((f32[60]{0:T(128)S(1)}, f32[60]{0:T(128)}, u32[]{:S(2)}) %copy-start.5) | copy-done | bytes 264
  30.7 0.1 fusion.1.carry_ref
  30.8 13.5 %exposures.1 = f32[2,512]{1,0:T(2,128)S(1)} custom-call(s32[512]{0:T(512)S(1)} %bitcast.27, s32[8192]{0:T(1024)S(1)} %bitcast.22, f32[16384]{0:T(1024)S(1)} %bitcast.20, f32[16384]{0:T(1024)S(1)} %bitcast.21, f32[1,512]{1,0:T(1,128)S(1)} %get-tuple-element.38.place_ref, f32[60,1024]{1,0:T(8,128)S(1)} %fusion.1.carry_ref, f32[60,1024]{1,0:T(8,128)S(1)} %fusion.2.first_ref, ...), custom_call_target="tpu_custom_call" | custom-call | tf_op jit(solution)/shard_map/exposures/pallas_call | solution.py:280
  44.3 1.6 %collective-permute-start.6 = (f32[2,512]{1,0:T(2,128)S(1)}, f32[2,512]{1,0:T(2,128)S(1)}, u32[]{:S(2)}, u32[]{:S(2)}) collective-permute-start(f32[2,512]{1,0:T(2,128)S(1)} %exposures.1), channel_id=1, source_target_pairs={{0,1},{1,0},{2,3},{3,2},{4,5},{5,4},{6,7},{7,6},{8,9},{9,8},{10,11... | collective-permute-start | bytes 12296 | tf_op jit(solution)/shard_map/ppermute | solution.py:28
  45.9 2.1 %collective-permute-done.6 = f32[2,512]{1,0:T(2,128)S(1)} collective-permute-done((f32[2,512]{1,0:T(2,128)S(1)}, f32[2,512]{1,0:T(2,128)S(1)}, u32[]{:S(2)}, u32[]{:S(2)}) %collective-permute-start.6) | collective-permute-done | bytes 4128 | tf_op jit(solution)/shard_map/ppermute | solution.py:28
  48.0 1.6 %collective-permute-start.7 = (f32[2,512]{1,0:T(2,128)S(1)}, f32[2,512]{1,0:T(2,128)S(1)}, u32[]{:S(2)}, u32[]{:S(2)}) collective-permute-start(f32[2,512]{1,0:T(2,128)S(1)} %add.49), channel_id=1, source_target_pairs={{0,2},{1,3},{2,0},{3,1},{4,6},{5,7},{6,4},{7,5},{8,10},{9,11},{10,... | collective-permute-start | bytes 12296 | tf_op jit(solution)/shard_map/ppermute | solution.py:28
  49.6 2.0 %collective-permute-done.7 = f32[2,512]{1,0:T(2,128)S(1)} collective-permute-done((f32[2,512]{1,0:T(2,128)S(1)}, f32[2,512]{1,0:T(2,128)S(1)}, u32[]{:S(2)}, u32[]{:S(2)}) %collective-permute-start.7) | collective-permute-done | bytes 4128 | tf_op jit(solution)/shard_map/ppermute | solution.py:28
  51.6 2.6 %collective-permute-start.8 = (f32[2,512]{1,0:T(2,128)S(1)}, f32[2,512]{1,0:T(2,128)S(1)}, u32[]{:S(2)}, u32[]{:S(2)}) collective-permute-start(f32[2,512]{1,0:T(2,128)S(1)} %add.50), channel_id=1, source_target_pairs={{0,4},{1,5},{2,6},{3,7},{4,0},{5,1},{6,2},{7,3},{8,12},{9,13},{10,... | collective-permute-start | bytes 12296 | tf_op jit(solution)/shard_map/ppermute | solution.py:28
  54.2 1.9 %collective-permute-done.8 = f32[2,512]{1,0:T(2,128)S(1)} collective-permute-done((f32[2,512]{1,0:T(2,128)S(1)}, f32[2,512]{1,0:T(2,128)S(1)}, u32[]{:S(2)}, u32[]{:S(2)}) %collective-permute-start.8) | collective-permute-done | bytes 4128 | tf_op jit(solution)/shard_map/ppermute | solution.py:28
  56.1 0.6 %add_multiply_fusion = f32[2,512]{1,0:T(2,128)} fusion(f32[2,512]{1,0:T(2,128)S(1)} %add.50, f32[2,512]{1,0:T(2,128)S(1)} %collective-permute-done.8), kind=kLoop, calls=%fused_computation.17 | loop fusion | flops 2048 | bytes 12288 | tf_op jit(solution)/shard_map/div | solution.py:358
  (8 shorter events, 0.1 us)
Async XLA Ops:
  0.0 15.7 %copy-start.4 = (f32[2,60,1024]{2,0,1:T(2,128)S(1)}, f32[2,60,1024]{2,0,1:T(2,128)}, u32[]{:S(2)}) copy-start(f32[2,60,1024]{2,0,1:T(2,128)} %param.8) | copy-start | bytes 1474564
  3.7 4.9 %collective-permute-start = (f32[60,128]{1,0:T(8,128)S(1)}, f32[60,128]{1,0:T(8,128)S(1)}, u32[]{:S(2)}, u32[]{:S(2)}) collective-permute-start(f32[60,128]{1,0:T(8,128)S(1)} %select_maximum_fusion), channel_id=1, source_target_pairs={{0,1},{1,0},{2,3},{3,2},{4,5},{5,4},{6,7},{7,6},{8,9},{9,8},{10,11... | collective-permute-start | bytes 92168 | tf_op jit(solution)/shard_map/ppermute | solution.py:28
  8.7 4.0 %collective-permute-start.1 = (f32[60,128]{1,0:T(8,128)S(1)}, f32[60,128]{1,0:T(8,128)S(1)}, u32[]{:S(2)}, u32[]{:S(2)}) collective-permute-start(f32[60,128]{1,0:T(8,128)S(1)} %fusion.14), channel_id=1, source_target_pairs={{0,2},{1,3},{2,0},{3,1},{4,6},{5,7},{6,4},{7,5},{8,10},{9,11},{10,... | collective-permute-start | bytes 92168 | tf_op jit(solution)/shard_map/ppermute | solution.py:28
  12.7 4.9 %collective-permute-start.2 = (f32[60,128]{1,0:T(8,128)S(1)}, f32[60,128]{1,0:T(8,128)S(1)}, u32[]{:S(2)}, u32[]{:S(2)}) collective-permute-start(f32[60,128]{1,0:T(8,128)S(1)} %add.43), channel_id=1, source_target_pairs={{0,4},{1,5},{2,6},{3,7},{4,0},{5,1},{6,2},{7,3},{8,12},{9,13},{10,... | collective-permute-start | bytes 92168 | tf_op jit(solution)/shard_map/ppermute | solution.py:28
  18.0 1.6 %collective-permute-start.3 = (f32[60,1024]{1,0:T(8,128)S(1)}, f32[60,1024]{1,0:T(8,128)S(1)}, u32[]{:S(2)}, u32[]{:S(2)}) collective-permute-start(f32[60,1024]{1,0:T(8,128)S(1)} %fusion.11.second_ref), channel_id=1, source_target_pairs={{0,8},{8,0},{16,24},{24,16},{1,9},{9,1},{17,25},{25,17},{2,10},{10... | collective-permute-start | bytes 737288 | tf_op jit(solution)/shard_map/ppermute | solution.py:314
  19.7 3.8 %copy-start = (s32[4096]{0:T(1024)S(1)}, s32[4096]{0:T(1024)}, u32[]{:S(2)}) copy-start(s32[4096]{0:T(1024)} %factor_hbm.1) | copy-start | bytes 49156
  19.7 3.8 %copy-start.1 = (s32[4096]{0:T(1024)S(1)}, s32[4096]{0:T(1024)}, u32[]{:S(2)}) copy-start(s32[4096]{0:T(1024)} %set_hbm.1) | copy-start | bytes 49156
  19.7 3.8 %copy-start.2 = (f32[4096]{0:T(1024)S(1)}, f32[4096]{0:T(1024)}, u32[]{:S(2)}) copy-start(f32[4096]{0:T(1024)} %notional_hbm.1) | copy-start | bytes 49156
  19.7 3.8 %copy-start.3 = (f32[4096]{0:T(1024)S(1)}, f32[4096]{0:T(1024)}, u32[]{:S(2)}) copy-start(f32[4096]{0:T(1024)} %strike_hbm.1) | copy-start | bytes 49156
  19.7 8.9 %collective-permute-start.4 = (f32[60,512]{1,0:T(8,128)S(1)}, f32[60,512]{1,0:T(8,128)S(1)}, u32[]{:S(2)}, u32[]{:S(2)}) collective-permute-start(f32[60,512]{1,0:T(8,128)S(1)} %slice_select_fusion), channel_id=1, source_target_pairs={{0,16},{8,24},{1,17},{9,25},{2,18},{10,26},{3,19},{11,27},{4,20},{... | collective-permute-start | bytes 368648 | tf_op jit(solution)/shard_map/ppermute | solution.py:319
  28.6 1.4 %collective-permute-start.5 = (f32[60,512]{1,0:T(8,128)S(1)}, f32[60,512]{1,0:T(8,128)S(1)}, u32[]{:S(2)}, u32[]{:S(2)}) collective-permute-start(f32[60,512]{1,0:T(8,128)S(1)} %collective-permute-done.4), channel_id=1, source_target_pairs={{0,8},{8,0},{16,24},{24,16},{1,9},{9,1},{17,25},{25,17},{2,10},{10... | collective-permute-start | bytes 368648 | tf_op jit(solution)/shard_map/ppermute | solution.py:321
  30.1 0.7 %copy-start.5 = (f32[60]{0:T(128)S(1)}, f32[60]{0:T(128)}, u32[]{:S(2)}) copy-start(f32[60]{0:T(128)} %param.10) | copy-start | bytes 724
  44.3 3.7 %collective-permute-start.6 = (f32[2,512]{1,0:T(2,128)S(1)}, f32[2,512]{1,0:T(2,128)S(1)}, u32[]{:S(2)}, u32[]{:S(2)}) collective-permute-start(f32[2,512]{1,0:T(2,128)S(1)} %exposures.1), channel_id=1, source_target_pairs={{0,1},{1,0},{2,3},{3,2},{4,5},{5,4},{6,7},{7,6},{8,9},{9,8},{10,11... | collective-permute-start | bytes 12296 | tf_op jit(solution)/shard_map/ppermute | solution.py:28
  48.0 3.6 %collective-permute-start.7 = (f32[2,512]{1,0:T(2,128)S(1)}, f32[2,512]{1,0:T(2,128)S(1)}, u32[]{:S(2)}, u32[]{:S(2)}) collective-permute-start(f32[2,512]{1,0:T(2,128)S(1)} %add.49), channel_id=1, source_target_pairs={{0,2},{1,3},{2,0},{3,1},{4,6},{5,7},{6,4},{7,5},{8,10},{9,11},{10,... | collective-permute-start | bytes 12296 | tf_op jit(solution)/shard_map/ppermute | solution.py:28
  51.6 4.5 %collective-permute-start.8 = (f32[2,512]{1,0:T(2,128)S(1)}, f32[2,512]{1,0:T(2,128)S(1)}, u32[]{:S(2)}, u32[]{:S(2)}) collective-permute-start(f32[2,512]{1,0:T(2,128)S(1)} %add.50), channel_id=1, source_target_pairs={{0,4},{1,5},{2,6},{3,7},{4,0},{5,1},{6,2},{7,3},{8,12},{9,13},{10,... | collective-permute-start | bytes 12296 | tf_op jit(solution)/shard_map/ppermute | solution.py:28

commit v3 on v2

--- a/solution.py
+++ b/solution.py
@@ -16,7 +16,7 @@
 PAIRS = ROWS // 2
 SHIFT = 16
 GROUP = 16
-PARTS = 4
+PARTS = 8
 
 
 def summed(part, axis):
@@ -197,17 +197,9 @@
 
     @pl.when(fits)
     def _():
-        def group(step, carry):
+        def group(step):
             first = (SETS // GROUP - 1 - step) * GROUP
             count = count_ref[first]
-            smaller = jnp.where(step == 0, -1, count_ref[jnp.minimum(first + GROUP, SETS - 1)])
-            for part, (_, both) in enumerate(copies):
-                needed = 2 * (PAIRS // PARTS) * part if part else -1
-
-                @pl.when((count > needed) & (smaller <= needed))
-                def _(both=both):
-                    for copy in both:
-                        copy.wait()
 
             def rows(r, nets):
                 nets = [list(n) for n in nets]
@@ -232,9 +224,21 @@
                     eight = [jnp.maximum(nets[date][part * 8 + i], 0.0) for i in range(8)]
                     at = pl.ds(pl.multiple_of(first + part * 8, 8), 8)
                     sum_ref[date, at, :] = over_sublanes(eight)
-            return carry
-
-        lax.fori_loop(0, SETS // GROUP, group, 0)
+            return step + 1
+
+        step = 0
+        for part, (wanted, both) in enumerate(copies):
+
+            @pl.when(wanted)
+            def _(both=both):
+                for copy in both:
+                    copy.wait()
+
+            def more(step, limit=2 * (PAIRS // PARTS) * (part + 1)):
+                last = jnp.maximum(SETS // GROUP - 1 - step, 0)
+                return (step < SETS // GROUP) & (count_ref[last * GROUP] <= limit)
+
+            step = lax.while_loop(more, group, step)
         ones = jnp.ones((8, LANES), jnp.bfloat16)
         lines = []
         for date in range(dates):
@@ -301,6 +305,29 @@
     )(count.reshape(SETS), index.reshape(-1), level.reshape(-1), weight.reshape(-1), place, before, first, second, *trades)
 
 
+def pack_kernel(owner_ref, cholesky_ref, out_ref):
+    dates, half = cholesky_ref.shape[0] // out_ref.shape[0], LANES // 2
+    factors = out_ref.shape[0]
+    section, holder = lax.axis_index("section"), lax.axis_index("paths")
+    out_ref[...] = jnp.zeros_like(out_ref)
+    for date in range(dates):
+        block = cholesky_ref[pl.ds(date * factors, factors), 0, :]
+        mine = owner_ref[section * dates + date] == holder
+        out_ref[:, date * half : date * half + factors] = jnp.where(mine, block, 0.0)
+
+
+def packed_blocks(cholesky, owner):
+    dates, _, factors, _ = cholesky.shape
+    return pl.pallas_call(
+        pack_kernel,
+        out_shape=jax.ShapeDtypeStruct((factors, LANES), jnp.float32),
+        in_specs=[pl.BlockSpec(memory_space=pltpu.SMEM), pl.BlockSpec(memory_space=pltpu.VMEM)],
+        out_specs=pl.BlockSpec(memory_space=pltpu.VMEM),
+        compiler_params=pltpu.CompilerParams(vmem_limit_bytes=4 << 20),
+        name="pack",
+    )(owner, cholesky.transpose(0, 2, 1, 3).reshape(dates * factors, 1, factors))
+
+
 def carried_in(total, fill):
     sections, section = lax.axis_size("section"), lax.axis_index("section")
     before = jnp.zeros_like(total)
@@ -330,13 +357,8 @@
 def shards(normal_draws, cholesky, log_spot, owner, trade_factor, trade_set, notional, strike):
     dates, factors, paths = normal_draws.shape
     half = LANES // 2
-    section = lax.axis_index("section")
     trades = (trade_factor, trade_set, notional, strike)
-    owners_here = lax.dynamic_slice_in_dim(owner, section * dates, dates)
-    mine = owners_here == lax.axis_index("paths")
-    spare = ((0, 0), (0, half - factors))
-    packed = [jnp.pad(jnp.where(mine[d], cholesky[d, 0], 0.0), spare) for d in range(dates)]
-    blocks = summed(jnp.concatenate(packed, axis=1), "paths")
+    blocks = summed(packed_blocks(cholesky, owner), "paths")
     draws = jnp.pad(normal_draws, ((0, 0), (0, half - factors), (0, 0))).reshape(dates * half, paths)
     first, second = (
         jnp.dot(
@@ -348,12 +370,13 @@
         for date in range(dates)
     )
 
-    def fill(ready, first=first):
-        ready, own, tied = lax.optimization_barrier((ready, first, trades))
+    def fill(ready):
+        spot = log_spot[:, None]
+        ready, *own, tied = lax.optimization_barrier((ready, first + spot, second + spot, trades))
         return ready, (own, tables(dates * paths // LANES, *tied))
 
-    before, (first, built) = carried_in(second, fill)
-    sums = exposures(built, before + log_spot[:, None], first, second, trades)
+    before, (levels, built) = carried_in(second, fill)
+    sums = exposures(built, before, *levels, trades)
     totals = summed(sums, "paths")
     return totals / (paths * lax.axis_size("paths"))
 

time: 57 us -> 54.1 us (0.949)
  other arithmetic: 3.86 us -> 0.79 us
  local copies, waits for them, and re-layouts: 1.54 us -> 3.39 us
  waiting for transfers between devices: 14 us -> 12.3 us
    unnamed x13 -> x15, local copies, waits for them, and re-layouts: 0.84 us -> 3.35 us
    slice x1 -> x0, other arithmetic: 1.49 us -> none  [shards(): cholesky[d, 0]]
    ppermute x6, waiting for transfers between devices: 11.5 us -> 10.5 us  [summed(): lax.ppermute(part, axis, [(i, i ^ distance) for i in range(size)])]
    eq x1 -> x0, other arithmetic: 0.79 us -> none  [shards(): mine = owners_here == lax.axis_index('paths')]
    ppermute x1, waiting for transfers between devices: 1.15 us -> 0.49 us  [carried_in(): got = lax.ppermute(total, 'section', pairs)]
    slice x1 -> x0, local copies, waits for them, and re-layouts: 0.66 us -> none  [shards(): mine[d]]
    select_n x1 -> x0, other arithmetic: 0.65 us -> none  [shards(): jnp.where(mine[d], cholesky[d, 0], 0.0)]
    pallas_call x0 -> x1, Pallas kernels: none -> 0.65 us  [packed_blocks(): pl.pallas_call(pack_kernel, out_shape=jax.ShapeDtypeStruct((factors, LANE...]
  transfers between devices with their start and end apart: 9 -> 9, of which waited for: 8 -> 8; matrix products, arithmetic and copies ran while one was open for 1% -> 3% of each run, Pallas kernels for 9% -> 9%
where the time goes in v3:
time: 54.1 us; the launch traced here: 53.9 us
  Pallas kernels  18.6 us (34%)
  starting transfers between devices  17.8 us (33%)
  waiting for transfers between devices  12.3 us (23%)
  local copies, waits for them, and re-layouts  3.39 us (6%)
  other arithmetic  0.79 us (1%)
  matrix products  0.79 us (1%)
    ppermute x6, starting transfers between devices, summed(): lax.ppermute(part, axis, [(i, i ^ distance) for i in range(size)])  13.9 us
    pallas_call x1, Pallas kernels, exposures(): pl.pallas_call(exposure_kernel, out_shape=jax.ShapeDtypeStruct((dates, SE...  12.9 us
    ppermute x6, waiting for transfers between devices, summed(): lax.ppermute(part, axis, [(i, i ^ distance) for i in range(size)])  10.5 us
    pallas_call x1, Pallas kernels, tables(): pl.pallas_call(functools.partial(table_kernel, step), out_shape=(jax.Shap...  5.09 us
    ppermute x1, starting transfers between devices, carried_in(): own = lax.ppermute(half, 'section', pairs)  3.74 us
    unnamed x15, local copies, waits for them, and re-layouts  3.35 us
    ppermute x1, waiting for transfers between devices, carried_in(): other = lax.ppermute(own, 'section', [(i, i ^ 1) for i in range(sections)])  1.33 us
  transfers between devices with their start and end apart: 9, of which 8 were waited for; matrix products, arithmetic and copies ran while one was open for 3% of the time, Pallas kernels for 9%

profile of v3, /device:TPU:0, one launch (start us, length us, event | category | flops | bytes accessed | tf_op | source)
XLA Modules:
  0.0 53.9 jit_solution(13698433889909232929)
XLA Ops:
  0.0 0.0 copy-start.5
  0.0 0.7 %copy-done.5 = s32[8]{0:T(128)S(1)} copy-done((s32[8]{0:T(128)S(1)}, s32[8]{0:T(128)}, u32[]{:S(2)}) %copy-start.5) | copy-done | bytes 56
  0.7 0.0 copy-start
  0.7 0.8 %copy-done = f32[2,1,60,60]{3,1,2,0:T(1,128)S(1)} copy-done((f32[2,1,60,60]{3,1,2,0:T(1,128)S(1)}, f32[2,1,60,60]{3,1,2,0:T(1,128)}, u32[]{:S(2)}) %copy-start) | copy-done | bytes 28824
  1.5 0.6 %pack.1 = f32[60,128]{1,0:T(8,128)S(1)} custom-call(s32[8]{0:T(128)S(1)} %copy-done.5, f32[120,1,60]{2,1,0:T(1,128)S(1)} %bitcast.17), custom_call_target="tpu_custom_call" | custom-call | tf_op jit(solution)/shard_map/pack/pallas_call | solution.py:321
  2.1 3.0 %collective-permute-start = (f32[60,128]{1,0:T(8,128)S(1)}, f32[60,128]{1,0:T(8,128)S(1)}, u32[]{:S(2)}, u32[]{:S(2)}) collective-permute-start(f32[60,128]{1,0:T(8,128)S(1)} %pack.1), channel_id=1, source_target_pairs={{0,1},{1,0},{2,3},{3,2},{4,5},{5,4},{6,7},{7,6},{8,9},{9,8},{10,11... | collective-permute-start | bytes 92168 | tf_op jit(solution)/shard_map/ppermute | solution.py:28
  5.2 1.9 %collective-permute-done = f32[60,128]{1,0:T(8,128)S(1)} collective-permute-done((f32[60,128]{1,0:T(8,128)S(1)}, f32[60,128]{1,0:T(8,128)S(1)}, u32[]{:S(2)}, u32[]{:S(2)}) %collective-permute-start) | collective-permute-done | bytes 30752 | tf_op jit(solution)/shard_map/ppermute | solution.py:28
  7.1 2.1 %collective-permute-start.1 = (f32[60,128]{1,0:T(8,128)S(1)}, f32[60,128]{1,0:T(8,128)S(1)}, u32[]{:S(2)}, u32[]{:S(2)}) collective-permute-start(f32[60,128]{1,0:T(8,128)S(1)} %add.40), channel_id=1, source_target_pairs={{0,2},{1,3},{2,0},{3,1},{4,6},{5,7},{6,4},{7,5},{8,10},{9,11},{10,... | collective-permute-start | bytes 92168 | tf_op jit(solution)/shard_map/ppermute | solution.py:28
  9.1 1.9 %collective-permute-done.1 = f32[60,128]{1,0:T(8,128)S(1)} collective-permute-done((f32[60,128]{1,0:T(8,128)S(1)}, f32[60,128]{1,0:T(8,128)S(1)}, u32[]{:S(2)}, u32[]{:S(2)}) %collective-permute-start.1) | collective-permute-done | bytes 30752 | tf_op jit(solution)/shard_map/ppermute | solution.py:28
  11.0 3.0 %collective-permute-start.2 = (f32[60,128]{1,0:T(8,128)S(1)}, f32[60,128]{1,0:T(8,128)S(1)}, u32[]{:S(2)}, u32[]{:S(2)}) collective-permute-start(f32[60,128]{1,0:T(8,128)S(1)} %add.41), channel_id=1, source_target_pairs={{0,4},{1,5},{2,6},{3,7},{4,0},{5,1},{6,2},{7,3},{8,12},{9,13},{10,... | collective-permute-start | bytes 92168 | tf_op jit(solution)/shard_map/ppermute | solution.py:28
  14.1 1.2 %copy.9 = f32[2,60,1024]{2,1,0:T(8,128)S(1)} copy(f32[2,60,1024]{2,0,1:T(2,128)} %param.8) | data formatting | bytes 983040 | tf_op args[0]
  15.3 0.7 %collective-permute-done.2 = f32[60,128]{1,0:T(8,128)S(1)} collective-permute-done((f32[60,128]{1,0:T(8,128)S(1)}, f32[60,128]{1,0:T(8,128)S(1)}, u32[]{:S(2)}, u32[]{:S(2)}) %collective-permute-start.2) | collective-permute-done | bytes 30752 | tf_op jit(solution)/shard_map/ppermute | solution.py:28
  16.0 0.4 fusion.6
  16.4 0.1 collective-permute-start.3
  16.5 0.0 copy-start.6
  16.5 0.6 %copy-done.6 = f32[60]{0:T(128)S(1)} copy-done((f32[60]{0:T(128)S(1)}, f32[60]{0:T(128)}, u32[]{:S(2)}) %copy-start.6) | copy-done | bytes 264
  17.2 0.4 convolution_add_fusion.first_ref
  17.5 0.5 collective-permute-done.3
  18.0 0.1 broadcast_add_fusion
  18.1 0.0 copy-start.1
  18.1 0.0 copy-start.2
  18.1 0.0 copy-start.3
  18.1 0.0 copy-start.4
  18.2 3.7 %collective-permute-start.4 = (f32[60,512]{1,0:T(8,128)S(1)}, f32[60,512]{1,0:T(8,128)S(1)}, u32[]{:S(2)}, u32[]{:S(2)}) collective-permute-start(f32[60,512]{1,0:T(8,128)S(1)} %slice_select_fusion), channel_id=1, source_target_pairs={{0,16},{8,24},{1,17},{9,25},{2,18},{10,26},{3,19},{11,27},{4,20},{... | collective-permute-start | bytes 368648 | tf_op jit(solution)/shard_map/ppermute | solution.py:346
  21.9 0.0 copy-done.1
  21.9 0.0 copy-done.2
  22.0 0.0 copy-done.3
  22.0 0.0 copy-done.4
  22.0 5.1 %tables.1 = (s32[16,4,128]{2,1,0:T(4,128)S(1)}, f32[16,8,128]{2,1,0:T(8,128)S(1)}, f32[16,8,128]{2,1,0:T(8,128)S(1)}, f32[1,512]{1,0:T(1,128)S(1)}, s32[1,512]{1,0:T(1,128)S(1)}) custom-call(s32[32,128]{1,0:T(8,128)S(1)} %bitcast.19, s32[32,128]{1,0:T(8,128)S(1)} %bitcast.20, f32[32,128]{1,0:T(8,128)S(1)} %bitcast.21, f32[32,128]{1,0:T(8,128)S(1)} %bitcast.22), custom_call_target="tpu_custom_call" | custom-call | flops 2097152000 | bytes 1048576 | tf_op jit(solution)/shard_map/tables/pallas_call | solution.py:130
  27.1 0.0 collective-permute-done.4
  27.1 0.1 collective-permute-start.5
  27.2 1.3 %collective-permute-done.5 = f32[60,512]{1,0:T(8,128)S(1)} collective-permute-done((f32[60,512]{1,0:T(8,128)S(1)}, f32[60,512]{1,0:T(8,128)S(1)}, u32[]{:S(2)}, u32[]{:S(2)}) %collective-permute-start.5) | collective-permute-done | bytes 122912 | tf_op jit(solution)/shard_map/ppermute | solution.py:348
  28.6 12.9 %exposures.1 = f32[2,512]{1,0:T(2,128)S(1)} custom-call(s32[512]{0:T(512)S(1)} %bitcast.23, s32[8192]{0:T(1024)S(1)} %bitcast.18, f32[16384]{0:T(1024)S(1)} %bitcast.15, f32[16384]{0:T(1024)S(1)} %bitcast.16, f32[1,512]{1,0:T(1,128)S(1)} %get-tuple-element.41.place_ref, f32[60,1024]{1,0:T(8,128)S(1)} %fusion.carry_ref, ...), custom_call_target="tpu_custom_call" | custom-call | tf_op jit(solution)/shard_map/exposures/pallas_call | solution.py:284
  41.5 1.6 %collective-permute-start.6 = (f32[2,512]{1,0:T(2,128)S(1)}, f32[2,512]{1,0:T(2,128)S(1)}, u32[]{:S(2)}, u32[]{:S(2)}) collective-permute-start(f32[2,512]{1,0:T(2,128)S(1)} %exposures.1), channel_id=1, source_target_pairs={{0,1},{1,0},{2,3},{3,2},{4,5},{5,4},{6,7},{7,6},{8,9},{9,8},{10,11... | collective-permute-start | bytes 12296 | tf_op jit(solution)/shard_map/ppermute | solution.py:28
  43.0 2.1 %collective-permute-done.6 = f32[2,512]{1,0:T(2,128)S(1)} collective-permute-done((f32[2,512]{1,0:T(2,128)S(1)}, f32[2,512]{1,0:T(2,128)S(1)}, u32[]{:S(2)}, u32[]{:S(2)}) %collective-permute-start.6) | collective-permute-done | bytes 4128 | tf_op jit(solution)/shard_map/ppermute | solution.py:28
  45.1 1.6 %collective-permute-start.7 = (f32[2,512]{1,0:T(2,128)S(1)}, f32[2,512]{1,0:T(2,128)S(1)}, u32[]{:S(2)}, u32[]{:S(2)}) collective-permute-start(f32[2,512]{1,0:T(2,128)S(1)} %add.48), channel_id=1, source_target_pairs={{0,2},{1,3},{2,0},{3,1},{4,6},{5,7},{6,4},{7,5},{8,10},{9,11},{10,... | collective-permute-start | bytes 12296 | tf_op jit(solution)/shard_map/ppermute | solution.py:28
  46.7 2.0 %collective-permute-done.7 = f32[2,512]{1,0:T(2,128)S(1)} collective-permute-done((f32[2,512]{1,0:T(2,128)S(1)}, f32[2,512]{1,0:T(2,128)S(1)}, u32[]{:S(2)}, u32[]{:S(2)}) %collective-permute-start.7) | collective-permute-done | bytes 4128 | tf_op jit(solution)/shard_map/ppermute | solution.py:28
  48.8 2.6 %collective-permute-start.8 = (f32[2,512]{1,0:T(2,128)S(1)}, f32[2,512]{1,0:T(2,128)S(1)}, u32[]{:S(2)}, u32[]{:S(2)}) collective-permute-start(f32[2,512]{1,0:T(2,128)S(1)} %add.49), channel_id=1, source_target_pairs={{0,4},{1,5},{2,6},{3,7},{4,0},{5,1},{6,2},{7,3},{8,12},{9,13},{10,... | collective-permute-start | bytes 12296 | tf_op jit(solution)/shard_map/ppermute | solution.py:28
  51.4 1.9 %collective-permute-done.8 = f32[2,512]{1,0:T(2,128)S(1)} collective-permute-done((f32[2,512]{1,0:T(2,128)S(1)}, f32[2,512]{1,0:T(2,128)S(1)}, u32[]{:S(2)}, u32[]{:S(2)}) %collective-permute-start.8) | collective-permute-done | bytes 4128 | tf_op jit(solution)/shard_map/ppermute | solution.py:28
  53.3 0.6 %add_multiply_fusion = f32[2,512]{1,0:T(2,128)} fusion(f32[2,512]{1,0:T(2,128)S(1)} %add.49, f32[2,512]{1,0:T(2,128)S(1)} %collective-permute-done.8), kind=kLoop, calls=%fused_computation.10 | loop fusion | flops 2048 | bytes 12288 | tf_op jit(solution)/shard_map/div | solution.py:381
  (9 shorter events, 0.1 us)
Async XLA Ops:
  0.0 0.7 %copy-start.5 = (s32[8]{0:T(128)S(1)}, s32[8]{0:T(128)}, u32[]{:S(2)}) copy-start(s32[8]{0:T(128)} %owner_ref.1) | copy-start | bytes 100
  0.7 0.8 %copy-start = (f32[2,1,60,60]{3,1,2,0:T(1,128)S(1)}, f32[2,1,60,60]{3,1,2,0:T(1,128)}, u32[]{:S(2)}) copy-start(f32[2,1,60,60]{3,1,2,0:T(1,128)} %param.9) | copy-start | bytes 86404
  2.1 4.9 %collective-permute-start = (f32[60,128]{1,0:T(8,128)S(1)}, f32[60,128]{1,0:T(8,128)S(1)}, u32[]{:S(2)}, u32[]{:S(2)}) collective-permute-start(f32[60,128]{1,0:T(8,128)S(1)} %pack.1), channel_id=1, source_target_pairs={{0,1},{1,0},{2,3},{3,2},{4,5},{5,4},{6,7},{7,6},{8,9},{9,8},{10,11... | collective-permute-start | bytes 92168 | tf_op jit(solution)/shard_map/ppermute | solution.py:28
  7.1 4.0 %collective-permute-start.1 = (f32[60,128]{1,0:T(8,128)S(1)}, f32[60,128]{1,0:T(8,128)S(1)}, u32[]{:S(2)}, u32[]{:S(2)}) collective-permute-start(f32[60,128]{1,0:T(8,128)S(1)} %add.40), channel_id=1, source_target_pairs={{0,2},{1,3},{2,0},{3,1},{4,6},{5,7},{6,4},{7,5},{8,10},{9,11},{10,... | collective-permute-start | bytes 92168 | tf_op jit(solution)/shard_map/ppermute | solution.py:28
  11.0 4.9 %collective-permute-start.2 = (f32[60,128]{1,0:T(8,128)S(1)}, f32[60,128]{1,0:T(8,128)S(1)}, u32[]{:S(2)}, u32[]{:S(2)}) collective-permute-start(f32[60,128]{1,0:T(8,128)S(1)} %add.41), channel_id=1, source_target_pairs={{0,4},{1,5},{2,6},{3,7},{4,0},{5,1},{6,2},{7,3},{8,12},{9,13},{10,... | collective-permute-start | bytes 92168 | tf_op jit(solution)/shard_map/ppermute | solution.py:28
  16.4 1.6 %collective-permute-start.3 = (f32[60,1024]{1,0:T(8,128)S(1)}, f32[60,1024]{1,0:T(8,128)S(1)}, u32[]{:S(2)}, u32[]{:S(2)}) collective-permute-start(f32[60,1024]{1,0:T(8,128)S(1)} %fusion.6), channel_id=1, source_target_pairs={{0,8},{8,0},{16,24},{24,16},{1,9},{9,1},{17,25},{25,17},{2,10},{10... | collective-permute-start | bytes 737288 | tf_op jit(solution)/shard_map/ppermute | solution.py:341
  16.5 0.7 %copy-start.6 = (f32[60]{0:T(128)S(1)}, f32[60]{0:T(128)}, u32[]{:S(2)}) copy-start(f32[60]{0:T(128)} %param.10) | copy-start | bytes 724
  18.1 3.8 %copy-start.1 = (s32[4096]{0:T(1024)S(1)}, s32[4096]{0:T(1024)}, u32[]{:S(2)}) copy-start(s32[4096]{0:T(1024)} %factor_hbm.1) | copy-start | bytes 49156
  18.1 3.8 %copy-start.2 = (s32[4096]{0:T(1024)S(1)}, s32[4096]{0:T(1024)}, u32[]{:S(2)}) copy-start(s32[4096]{0:T(1024)} %set_hbm.1) | copy-start | bytes 49156
  18.1 3.8 %copy-start.3 = (f32[4096]{0:T(1024)S(1)}, f32[4096]{0:T(1024)}, u32[]{:S(2)}) copy-start(f32[4096]{0:T(1024)} %notional_hbm.1) | copy-start | bytes 49156
  18.1 3.8 %copy-start.4 = (f32[4096]{0:T(1024)S(1)}, f32[4096]{0:T(1024)}, u32[]{:S(2)}) copy-start(f32[4096]{0:T(1024)} %strike_hbm.1) | copy-start | bytes 49156
  18.2 8.9 %collective-permute-start.4 = (f32[60,512]{1,0:T(8,128)S(1)}, f32[60,512]{1,0:T(8,128)S(1)}, u32[]{:S(2)}, u32[]{:S(2)}) collective-permute-start(f32[60,512]{1,0:T(8,128)S(1)} %slice_select_fusion), channel_id=1, source_target_pairs={{0,16},{8,24},{1,17},{9,25},{2,18},{10,26},{3,19},{11,27},{4,20},{... | collective-permute-start | bytes 368648 | tf_op jit(solution)/shard_map/ppermute | solution.py:346
  27.1 1.4 %collective-permute-start.5 = (f32[60,512]{1,0:T(8,128)S(1)}, f32[60,512]{1,0:T(8,128)S(1)}, u32[]{:S(2)}, u32[]{:S(2)}) collective-permute-start(f32[60,512]{1,0:T(8,128)S(1)} %collective-permute-done.4), channel_id=1, source_target_pairs={{0,8},{8,0},{16,24},{24,16},{1,9},{9,1},{17,25},{25,17},{2,10},{10... | collective-permute-start | bytes 368648 | tf_op jit(solution)/shard_map/ppermute | solution.py:348
  41.5 3.7 %collective-permute-start.6 = (f32[2,512]{1,0:T(2,128)S(1)}, f32[2,512]{1,0:T(2,128)S(1)}, u32[]{:S(2)}, u32[]{:S(2)}) collective-permute-start(f32[2,512]{1,0:T(2,128)S(1)} %exposures.1), channel_id=1, source_target_pairs={{0,1},{1,0},{2,3},{3,2},{4,5},{5,4},{6,7},{7,6},{8,9},{9,8},{10,11... | collective-permute-start | bytes 12296 | tf_op jit(solution)/shard_map/ppermute | solution.py:28
  45.1 3.6 %collective-permute-start.7 = (f32[2,512]{1,0:T(2,128)S(1)}, f32[2,512]{1,0:T(2,128)S(1)}, u32[]{:S(2)}, u32[]{:S(2)}) collective-permute-start(f32[2,512]{1,0:T(2,128)S(1)} %add.48), channel_id=1, source_target_pairs={{0,2},{1,3},{2,0},{3,1},{4,6},{5,7},{6,4},{7,5},{8,10},{9,11},{10,... | collective-permute-start | bytes 12296 | tf_op jit(solution)/shard_map/ppermute | solution.py:28
  48.8 4.5 %collective-permute-start.8 = (f32[2,512]{1,0:T(2,128)S(1)}, f32[2,512]{1,0:T(2,128)S(1)}, u32[]{:S(2)}, u32[]{:S(2)}) collective-permute-start(f32[2,512]{1,0:T(2,128)S(1)} %add.49), channel_id=1, source_target_pairs={{0,4},{1,5},{2,6},{3,7},{4,0},{5,1},{6,2},{7,3},{8,12},{9,13},{10,... | collective-permute-start | bytes 12296 | tf_op jit(solution)/shard_map/ppermute | solution.py:28

commit v4 on v3

--- a/solution.py
+++ b/solution.py
@@ -23,11 +23,17 @@
     size = lax.axis_size(axis)
     if size & (size - 1):
         return lax.psum(part, axis)
-    distance = 1
-    while distance < size:
-        part = part + lax.ppermute(part, axis, [(i, i ^ distance) for i in range(size)])
-        distance *= 2
-    return part
+
+    def swapped(distance):
+        return lax.ppermute(part, axis, [(i, i ^ distance) for i in range(size)])
+
+    distance = size // 2
+    while distance > 2:
+        part = part + swapped(distance)
+        distance //= 2
+    if size >= 4:
+        return (part + swapped(1)) + (swapped(2) + swapped(3))
+    return part + swapped(1) if size == 2 else part
 
 
 def pieces(value):

time: 54.1 us -> 51.6 us (0.954)
  waiting for transfers between devices: 12.3 us -> 10.6 us
  starting transfers between devices: 17.8 us -> 17.1 us
    ppermute x6 -> x8, waiting for transfers between devices: 10.5 us -> 8.83 us  [swapped(): return lax.ppermute(part, axis, [(i, i ^ distance) for i in range(size)])]
    ppermute x6 -> x8, starting transfers between devices: 13.9 us -> 13.5 us  [swapped(): return lax.ppermute(part, axis, [(i, i ^ distance) for i in range(size)])]
  transfers between devices with their start and end apart: 9 -> 11, of which waited for: 8 -> 10; matrix products, arithmetic and copies ran while one was open for 3% -> 3% of each run, Pallas kernels for 9% -> 10%
where the time goes in v4:
time: 51.6 us; the launch traced here: 51.4 us
  Pallas kernels  18.5 us (36%)
  starting transfers between devices  17.1 us (33%)
  waiting for transfers between devices  10.6 us (21%)
  local copies, waits for them, and re-layouts  3.39 us (7%)
  matrix products  0.8 us (2%)
  other arithmetic  0.79 us (2%)
    ppermute x8, starting transfers between devices, swapped(): return lax.ppermute(part, axis, [(i, i ^ distance) for i in range(size)])  13.5 us
    pallas_call x1, Pallas kernels, exposures(): pl.pallas_call(exposure_kernel, out_shape=jax.ShapeDtypeStruct((dates, SE...  12.8 us
    ppermute x8, waiting for transfers between devices, swapped(): return lax.ppermute(part, axis, [(i, i ^ distance) for i in range(size)])  8.83 us
    pallas_call x1, Pallas kernels, tables(): pl.pallas_call(functools.partial(table_kernel, step), out_shape=(jax.Shap...  5.09 us
    ppermute x1, starting transfers between devices, carried_in(): own = lax.ppermute(half, 'section', pairs)  3.4 us
    unnamed x15, local copies, waits for them, and re-layouts  3.35 us
    ppermute x1, waiting for transfers between devices, carried_in(): other = lax.ppermute(own, 'section', [(i, i ^ 1) for i in range(sections)])  1.33 us
  transfers between devices with their start and end apart: 11, of which 10 were waited for; matrix products, arithmetic and copies ran while one was open for 3% of the time, Pallas kernels for 10%

profile of v4, /device:TPU:0, one launch (start us, length us, event | category | flops | bytes accessed | tf_op | source)
XLA Modules:
  0.0 51.4 jit_solution(8158536501329241801)
XLA Ops:
  0.0 0.0 copy-start.5
  0.0 0.7 %copy-done.5 = s32[8]{0:T(128)S(1)} copy-done((s32[8]{0:T(128)S(1)}, s32[8]{0:T(128)}, u32[]{:S(2)}) %copy-start.5) | copy-done | bytes 56
  0.7 0.0 copy-start
  0.7 0.8 %copy-done = f32[2,1,60,60]{3,1,2,0:T(1,128)S(1)} copy-done((f32[2,1,60,60]{3,1,2,0:T(1,128)S(1)}, f32[2,1,60,60]{3,1,2,0:T(1,128)}, u32[]{:S(2)}) %copy-start) | copy-done | bytes 28824
  1.5 0.6 %pack.1 = f32[60,128]{1,0:T(8,128)S(1)} custom-call(s32[8]{0:T(128)S(1)} %copy-done.5, f32[120,1,60]{2,1,0:T(1,128)S(1)} %bitcast.17), custom_call_target="tpu_custom_call" | custom-call | tf_op jit(solution)/shard_map/pack/pallas_call | solution.py:327
  2.1 4.1 %collective-permute-start = (f32[60,128]{1,0:T(8,128)S(1)}, f32[60,128]{1,0:T(8,128)S(1)}, u32[]{:S(2)}, u32[]{:S(2)}) collective-permute-start(f32[60,128]{1,0:T(8,128)S(1)} %pack.1), channel_id=1, source_target_pairs={{0,4},{1,5},{2,6},{3,7},{4,0},{5,1},{6,2},{7,3},{8,12},{9,13},{10,... | collective-permute-start | bytes 92168 | tf_op jit(solution)/shard_map/ppermute | solution.py:28
  6.2 2.2 %collective-permute-done = f32[60,128]{1,0:T(8,128)S(1)} collective-permute-done((f32[60,128]{1,0:T(8,128)S(1)}, f32[60,128]{1,0:T(8,128)S(1)}, u32[]{:S(2)}, u32[]{:S(2)}) %collective-permute-start) | collective-permute-done | bytes 30752 | tf_op jit(solution)/shard_map/ppermute | solution.py:28
  8.5 2.5 %collective-permute-start.3 = (f32[60,128]{1,0:T(8,128)S(1)}, f32[60,128]{1,0:T(8,128)S(1)}, u32[]{:S(2)}, u32[]{:S(2)}) collective-permute-start(f32[60,128]{1,0:T(8,128)S(1)} %add.46), channel_id=1, source_target_pairs={{0,3},{1,2},{2,1},{3,0},{4,7},{5,6},{6,5},{7,4},{8,11},{9,10},{10,... | collective-permute-start | bytes 92168 | tf_op jit(solution)/shard_map/ppermute | solution.py:28
  11.0 0.7 %collective-permute-start.2 = (f32[60,128]{1,0:T(8,128)S(1)}, f32[60,128]{1,0:T(8,128)S(1)}, u32[]{:S(2)}, u32[]{:S(2)}) collective-permute-start(f32[60,128]{1,0:T(8,128)S(1)} %add.46), channel_id=1, source_target_pairs={{0,2},{1,3},{2,0},{3,1},{4,6},{5,7},{6,4},{7,5},{8,10},{9,11},{10,... | collective-permute-start | bytes 92168 | tf_op jit(solution)/shard_map/ppermute | solution.py:28
  11.7 0.3 collective-permute-start.1
  12.0 1.2 %copy.9 = f32[2,60,1024]{2,1,0:T(8,128)S(1)} copy(f32[2,60,1024]{2,0,1:T(2,128)} %param.8) | data formatting | bytes 983040 | tf_op args[0]
  13.2 0.1 collective-permute-done.3
  13.3 1.6 %collective-permute-done.2 = f32[60,128]{1,0:T(8,128)S(1)} collective-permute-done((f32[60,128]{1,0:T(8,128)S(1)}, f32[60,128]{1,0:T(8,128)S(1)}, u32[]{:S(2)}, u32[]{:S(2)}) %collective-permute-start.2) | collective-permute-done | bytes 30752 | tf_op jit(solution)/shard_map/ppermute | solution.py:28
  14.9 0.7 %collective-permute-done.1 = f32[60,128]{1,0:T(8,128)S(1)} collective-permute-done((f32[60,128]{1,0:T(8,128)S(1)}, f32[60,128]{1,0:T(8,128)S(1)}, u32[]{:S(2)}, u32[]{:S(2)}) %collective-permute-start.1) | collective-permute-done | bytes 30752 | tf_op jit(solution)/shard_map/ppermute | solution.py:28
  15.6 0.4 fusion.6
  16.1 0.1 collective-permute-start.4
  16.1 0.0 copy-start.6
  16.2 0.6 %copy-done.6 = f32[60]{0:T(128)S(1)} copy-done((f32[60]{0:T(128)S(1)}, f32[60]{0:T(128)}, u32[]{:S(2)}) %copy-start.6) | copy-done | bytes 264
  16.8 0.4 convolution_add_fusion.first_ref
  17.2 0.5 collective-permute-done.4
  17.7 0.1 broadcast_add_fusion
  17.7 0.0 copy-start.1
  17.8 0.0 copy-start.2
  17.8 0.0 copy-start.3
  17.8 0.0 copy-start.4
  17.8 3.4 %collective-permute-start.5 = (f32[60,512]{1,0:T(8,128)S(1)}, f32[60,512]{1,0:T(8,128)S(1)}, u32[]{:S(2)}, u32[]{:S(2)}) collective-permute-start(f32[60,512]{1,0:T(8,128)S(1)} %slice_select_fusion), channel_id=1, source_target_pairs={{0,16},{8,24},{1,17},{9,25},{2,18},{10,26},{3,19},{11,27},{4,20},{... | collective-permute-start | bytes 368648 | tf_op jit(solution)/shard_map/ppermute | solution.py:352
  21.2 0.0 copy-done.1
  21.2 0.0 copy-done.2
  21.2 0.0 copy-done.3
  21.3 0.0 copy-done.4
  21.3 5.1 %tables.1 = (s32[16,4,128]{2,1,0:T(4,128)S(1)}, f32[16,8,128]{2,1,0:T(8,128)S(1)}, f32[16,8,128]{2,1,0:T(8,128)S(1)}, f32[1,512]{1,0:T(1,128)S(1)}, s32[1,512]{1,0:T(1,128)S(1)}) custom-call(s32[32,128]{1,0:T(8,128)S(1)} %bitcast.19, s32[32,128]{1,0:T(8,128)S(1)} %bitcast.20, f32[32,128]{1,0:T(8,128)S(1)} %bitcast.21, f32[32,128]{1,0:T(8,128)S(1)} %bitcast.22), custom_call_target="tpu_custom_call" | custom-call | flops 2097152000 | bytes 1048576 | tf_op jit(solution)/shard_map/tables/pallas_call | solution.py:136
  26.4 0.0 collective-permute-done.5
  26.4 0.1 collective-permute-start.6
  26.5 1.3 %collective-permute-done.6 = f32[60,512]{1,0:T(8,128)S(1)} collective-permute-done((f32[60,512]{1,0:T(8,128)S(1)}, f32[60,512]{1,0:T(8,128)S(1)}, u32[]{:S(2)}, u32[]{:S(2)}) %collective-permute-start.6) | collective-permute-done | bytes 122912 | tf_op jit(solution)/shard_map/ppermute | solution.py:354
  27.9 12.8 %exposures.1 = f32[2,512]{1,0:T(2,128)S(1)} custom-call(s32[512]{0:T(512)S(1)} %bitcast.23, s32[8192]{0:T(1024)S(1)} %bitcast.18, f32[16384]{0:T(1024)S(1)} %bitcast.15, f32[16384]{0:T(1024)S(1)} %bitcast.16, f32[1,512]{1,0:T(1,128)S(1)} %get-tuple-element.41.place_ref, f32[60,1024]{1,0:T(8,128)S(1)} %fusion.carry_ref, ...), custom_call_target="tpu_custom_call" | custom-call | tf_op jit(solution)/shard_map/exposures/pallas_call | solution.py:290
  40.6 2.4 %collective-permute-start.7 = (f32[2,512]{1,0:T(2,128)S(1)}, f32[2,512]{1,0:T(2,128)S(1)}, u32[]{:S(2)}, u32[]{:S(2)}) collective-permute-start(f32[2,512]{1,0:T(2,128)S(1)} %exposures.1), channel_id=1, source_target_pairs={{0,4},{1,5},{2,6},{3,7},{4,0},{5,1},{6,2},{7,3},{8,12},{9,13},{10,... | collective-permute-start | bytes 12296 | tf_op jit(solution)/shard_map/ppermute | solution.py:28
  43.1 2.1 %collective-permute-done.7 = f32[2,512]{1,0:T(2,128)S(1)} collective-permute-done((f32[2,512]{1,0:T(2,128)S(1)}, f32[2,512]{1,0:T(2,128)S(1)}, u32[]{:S(2)}, u32[]{:S(2)}) %collective-permute-start.7) | collective-permute-done | bytes 4128 | tf_op jit(solution)/shard_map/ppermute | solution.py:28
  45.2 1.3 %collective-permute-start.10 = (f32[2,512]{1,0:T(2,128)S(1)}, f32[2,512]{1,0:T(2,128)S(1)}, u32[]{:S(2)}, u32[]{:S(2)}) collective-permute-start(f32[2,512]{1,0:T(2,128)S(1)} %add.55), channel_id=1, source_target_pairs={{0,3},{1,2},{2,1},{3,0},{4,7},{5,6},{6,5},{7,4},{8,11},{9,10},{10,... | collective-permute-start | bytes 12296 | tf_op jit(solution)/shard_map/ppermute | solution.py:28
  46.5 0.7 %collective-permute-start.9 = (f32[2,512]{1,0:T(2,128)S(1)}, f32[2,512]{1,0:T(2,128)S(1)}, u32[]{:S(2)}, u32[]{:S(2)}) collective-permute-start(f32[2,512]{1,0:T(2,128)S(1)} %add.55), channel_id=1, source_target_pairs={{0,2},{1,3},{2,0},{3,1},{4,6},{5,7},{6,4},{7,5},{8,10},{9,11},{10,... | collective-permute-start | bytes 12296 | tf_op jit(solution)/shard_map/ppermute | solution.py:28
  47.2 1.5 %collective-permute-start.8 = (f32[2,512]{1,0:T(2,128)S(1)}, f32[2,512]{1,0:T(2,128)S(1)}, u32[]{:S(2)}, u32[]{:S(2)}) collective-permute-start(f32[2,512]{1,0:T(2,128)S(1)} %add.55), channel_id=1, source_target_pairs={{0,1},{1,0},{2,3},{3,2},{4,5},{5,4},{6,7},{7,6},{8,9},{9,8},{10,11... | collective-permute-start | bytes 12296 | tf_op jit(solution)/shard_map/ppermute | solution.py:28
  48.7 1.0 %collective-permute-done.10 = f32[2,512]{1,0:T(2,128)S(1)} collective-permute-done((f32[2,512]{1,0:T(2,128)S(1)}, f32[2,512]{1,0:T(2,128)S(1)}, u32[]{:S(2)}, u32[]{:S(2)}) %collective-permute-start.10) | collective-permute-done | bytes 4128 | tf_op jit(solution)/shard_map/ppermute | solution.py:28
  49.7 0.4 collective-permute-done.9
  50.1 0.7 %collective-permute-done.8 = f32[2,512]{1,0:T(2,128)S(1)} collective-permute-done((f32[2,512]{1,0:T(2,128)S(1)}, f32[2,512]{1,0:T(2,128)S(1)}, u32[]{:S(2)}, u32[]{:S(2)}) %collective-permute-start.8) | collective-permute-done | bytes 4128 | tf_op jit(solution)/shard_map/ppermute | solution.py:28
  50.8 0.6 %add_multiply_fusion = f32[2,512]{1,0:T(2,128)} fusion(f32[2,512]{1,0:T(2,128)S(1)} %collective-permute-done.9, f32[2,512]{1,0:T(2,128)S(1)} %collective-permute-done.10, f32[2,512]{1,0:T(2,128)S(1)} %add.55, f32[2,512]{1,0:T(2,128)S(1)} %collective-permute-done.8), kind=kLoop, calls=%fused_computation.11 | loop fusion | flops 4096 | bytes 20480 | tf_op jit(solution)/shard_map/div | solution.py:387
  (7 shorter events, 0.1 us)
Async XLA Ops:
  0.0 0.7 %copy-start.5 = (s32[8]{0:T(128)S(1)}, s32[8]{0:T(128)}, u32[]{:S(2)}) copy-start(s32[8]{0:T(128)} %owner_ref.1) | copy-start | bytes 100
  0.7 0.8 %copy-start = (f32[2,1,60,60]{3,1,2,0:T(1,128)S(1)}, f32[2,1,60,60]{3,1,2,0:T(1,128)}, u32[]{:S(2)}) copy-start(f32[2,1,60,60]{3,1,2,0:T(1,128)} %param.9) | copy-start | bytes 86404
  2.1 6.4 %collective-permute-start = (f32[60,128]{1,0:T(8,128)S(1)}, f32[60,128]{1,0:T(8,128)S(1)}, u32[]{:S(2)}, u32[]{:S(2)}) collective-permute-start(f32[60,128]{1,0:T(8,128)S(1)} %pack.1), channel_id=1, source_target_pairs={{0,4},{1,5},{2,6},{3,7},{4,0},{5,1},{6,2},{7,3},{8,12},{9,13},{10,... | collective-permute-start | bytes 92168 | tf_op jit(solution)/shard_map/ppermute | solution.py:28
  8.5 4.8 %collective-permute-start.3 = (f32[60,128]{1,0:T(8,128)S(1)}, f32[60,128]{1,0:T(8,128)S(1)}, u32[]{:S(2)}, u32[]{:S(2)}) collective-permute-start(f32[60,128]{1,0:T(8,128)S(1)} %add.46), channel_id=1, source_target_pairs={{0,3},{1,2},{2,1},{3,0},{4,7},{5,6},{6,5},{7,4},{8,11},{9,10},{10,... | collective-permute-start | bytes 92168 | tf_op jit(solution)/shard_map/ppermute | solution.py:28
  11.0 3.9 %collective-permute-start.2 = (f32[60,128]{1,0:T(8,128)S(1)}, f32[60,128]{1,0:T(8,128)S(1)}, u32[]{:S(2)}, u32[]{:S(2)}) collective-permute-start(f32[60,128]{1,0:T(8,128)S(1)} %add.46), channel_id=1, source_target_pairs={{0,2},{1,3},{2,0},{3,1},{4,6},{5,7},{6,4},{7,5},{8,10},{9,11},{10,... | collective-permute-start | bytes 92168 | tf_op jit(solution)/shard_map/ppermute | solution.py:28
  11.7 3.9 %collective-permute-start.1 = (f32[60,128]{1,0:T(8,128)S(1)}, f32[60,128]{1,0:T(8,128)S(1)}, u32[]{:S(2)}, u32[]{:S(2)}) collective-permute-start(f32[60,128]{1,0:T(8,128)S(1)} %add.46), channel_id=1, source_target_pairs={{0,1},{1,0},{2,3},{3,2},{4,5},{5,4},{6,7},{7,6},{8,9},{9,8},{10,11... | collective-permute-start | bytes 92168 | tf_op jit(solution)/shard_map/ppermute | solution.py:28
  16.1 1.6 %collective-permute-start.4 = (f32[60,1024]{1,0:T(8,128)S(1)}, f32[60,1024]{1,0:T(8,128)S(1)}, u32[]{:S(2)}, u32[]{:S(2)}) collective-permute-start(f32[60,1024]{1,0:T(8,128)S(1)} %fusion.6), channel_id=1, source_target_pairs={{0,8},{8,0},{16,24},{24,16},{1,9},{9,1},{17,25},{25,17},{2,10},{10... | collective-permute-start | bytes 737288 | tf_op jit(solution)/shard_map/ppermute | solution.py:347
  16.1 0.7 %copy-start.6 = (f32[60]{0:T(128)S(1)}, f32[60]{0:T(128)}, u32[]{:S(2)}) copy-start(f32[60]{0:T(128)} %param.10) | copy-start | bytes 724
  17.7 3.5 %copy-start.1 = (s32[4096]{0:T(1024)S(1)}, s32[4096]{0:T(1024)}, u32[]{:S(2)}) copy-start(s32[4096]{0:T(1024)} %factor_hbm.1) | copy-start | bytes 49156
  17.8 3.5 %copy-start.2 = (s32[4096]{0:T(1024)S(1)}, s32[4096]{0:T(1024)}, u32[]{:S(2)}) copy-start(s32[4096]{0:T(1024)} %set_hbm.1) | copy-start | bytes 49156
  17.8 3.5 %copy-start.3 = (f32[4096]{0:T(1024)S(1)}, f32[4096]{0:T(1024)}, u32[]{:S(2)}) copy-start(f32[4096]{0:T(1024)} %notional_hbm.1) | copy-start | bytes 49156
  17.8 3.5 %copy-start.4 = (f32[4096]{0:T(1024)S(1)}, f32[4096]{0:T(1024)}, u32[]{:S(2)}) copy-start(f32[4096]{0:T(1024)} %strike_hbm.1) | copy-start | bytes 49156
  17.8 8.5 %collective-permute-start.5 = (f32[60,512]{1,0:T(8,128)S(1)}, f32[60,512]{1,0:T(8,128)S(1)}, u32[]{:S(2)}, u32[]{:S(2)}) collective-permute-start(f32[60,512]{1,0:T(8,128)S(1)} %slice_select_fusion), channel_id=1, source_target_pairs={{0,16},{8,24},{1,17},{9,25},{2,18},{10,26},{3,19},{11,27},{4,20},{... | collective-permute-start | bytes 368648 | tf_op jit(solution)/shard_map/ppermute | solution.py:352
  26.4 1.4 %collective-permute-start.6 = (f32[60,512]{1,0:T(8,128)S(1)}, f32[60,512]{1,0:T(8,128)S(1)}, u32[]{:S(2)}, u32[]{:S(2)}) collective-permute-start(f32[60,512]{1,0:T(8,128)S(1)} %collective-permute-done.5), channel_id=1, source_target_pairs={{0,8},{8,0},{16,24},{24,16},{1,9},{9,1},{17,25},{25,17},{2,10},{10... | collective-permute-start | bytes 368648 | tf_op jit(solution)/shard_map/ppermute | solution.py:354
  40.6 4.6 %collective-permute-start.7 = (f32[2,512]{1,0:T(2,128)S(1)}, f32[2,512]{1,0:T(2,128)S(1)}, u32[]{:S(2)}, u32[]{:S(2)}) collective-permute-start(f32[2,512]{1,0:T(2,128)S(1)} %exposures.1), channel_id=1, source_target_pairs={{0,4},{1,5},{2,6},{3,7},{4,0},{5,1},{6,2},{7,3},{8,12},{9,13},{10,... | collective-permute-start | bytes 12296 | tf_op jit(solution)/shard_map/ppermute | solution.py:28
  45.2 4.5 %collective-permute-start.10 = (f32[2,512]{1,0:T(2,128)S(1)}, f32[2,512]{1,0:T(2,128)S(1)}, u32[]{:S(2)}, u32[]{:S(2)}) collective-permute-start(f32[2,512]{1,0:T(2,128)S(1)} %add.55), channel_id=1, source_target_pairs={{0,3},{1,2},{2,1},{3,0},{4,7},{5,6},{6,5},{7,4},{8,11},{9,10},{10,... | collective-permute-start | bytes 12296 | tf_op jit(solution)/shard_map/ppermute | solution.py:28
  46.5 3.6 %collective-permute-start.9 = (f32[2,512]{1,0:T(2,128)S(1)}, f32[2,512]{1,0:T(2,128)S(1)}, u32[]{:S(2)}, u32[]{:S(2)}) collective-permute-start(f32[2,512]{1,0:T(2,128)S(1)} %add.55), channel_id=1, source_target_pairs={{0,2},{1,3},{2,0},{3,1},{4,6},{5,7},{6,4},{7,5},{8,10},{9,11},{10,... | collective-permute-start | bytes 12296 | tf_op jit(solution)/shard_map/ppermute | solution.py:28
  47.2 3.6 %collective-permute-start.8 = (f32[2,512]{1,0:T(2,128)S(1)}, f32[2,512]{1,0:T(2,128)S(1)}, u32[]{:S(2)}, u32[]{:S(2)}) collective-permute-start(f32[2,512]{1,0:T(2,128)S(1)} %add.55), channel_id=1, source_target_pairs={{0,1},{1,0},{2,3},{3,2},{4,5},{5,4},{6,7},{7,6},{8,9},{9,8},{10,11... | collective-permute-start | bytes 12296 | tf_op jit(solution)/shard_map/ppermute | solution.py:28

commit v5 on v4

--- a/solution.py
+++ b/solution.py
@@ -111,7 +111,7 @@
         places.append(jnp.sum(jnp.where(ahead, 1.0, 0.0), axis=0, keepdims=True))
     place = jnp.concatenate(places, axis=1)
     moved = moves(place)
-    place_ref[...] = place
+    place_ref[...] = moved
     table = dot_last(table[: 7 * ROWS, :].astype(jnp.bfloat16), moved)
     index = table[:ROWS, :].astype(jnp.int32)
     index = (index[:PAIRS] + (index[PAIRS:] << SHIFT)) * step
@@ -139,7 +139,7 @@
             jax.ShapeDtypeStruct((PAIRS, BLOCKS, LANES), jnp.int32),
             jax.ShapeDtypeStruct((PAIRS, 2 * BLOCKS, LANES), jnp.float32),
             jax.ShapeDtypeStruct((PAIRS, 2 * BLOCKS, LANES), jnp.float32),
-            jax.ShapeDtypeStruct((1, SETS), jnp.float32),
+            jax.ShapeDtypeStruct((SETS, SETS), jnp.bfloat16),
             jax.ShapeDtypeStruct((1, SETS), jnp.int32),
         ),
         in_specs=[vmem] * 4,
@@ -169,37 +169,47 @@
 
 
 def exposure_kernel(
-    count_ref, index_hbm, level_hbm, weight_hbm, place_ref, carry_ref, first_ref, second_ref,
+    count_hbm, index_hbm, level_hbm, weight_hbm, place_ref, carry_ref, first_ref, second_ref,
     factor_hbm, set_hbm, notional_hbm, strike_hbm,
     out_ref,
-    index_ref, limit_ref, weight_ref, copied, level_ref, price_ref, sum_ref, net_ref, factor_s, set_s, notional_s, strike_s,
+    count_ref, index_ref, limit_ref, weight_ref, counted, copied, level_ref, price_ref, sum_ref, net_ref, factor_s, set_s, notional_s, strike_s,
 ):
     own_refs = (first_ref, second_ref)
     dates, (factors, paths) = len(own_refs), first_ref.shape
     tiles = paths // LANES
-    largest = count_ref[0]
-    fits = largest <= ROWS
+    counting = pltpu.make_async_copy(count_hbm, count_ref, counted)
+    counting.start()
     copies = []
     for part in range(PARTS):
         each = PAIRS // PARTS
-        wanted = fits & ((largest > 2 * each * part) | (part == 0))
         both = []
-        for source, target, row in ((index_hbm, index_ref, SETS), (level_hbm, limit_ref, 2 * SETS), (weight_hbm, weight_ref, 2 * SETS)):
+        for source, target, row in (
+            (index_hbm, index_ref, SETS), (level_hbm, limit_ref, 2 * SETS), (weight_hbm, weight_ref, 2 * SETS)
+        ):
             at = pl.ds(part * each * row, each * row)
             both.append(pltpu.make_async_copy(source.at[at], target.at[at], copied.at[part, len(both)]))
-        copies.append((wanted, both))
-
-        @pl.when(wanted)
-        def _(both=both):
-            for copy in both:
-                copy.start()
-
+        copies.append(both)
+    for copy in copies[0]:
+        copy.start()
     stacked_ref = price_ref.reshape(factors, dates, tiles, LANES)
     carried = carry_ref[...]
     for date in range(dates):
         level = jnp.exp(carried + own_refs[date][...])
         level_ref[date] = level
         stacked_ref[:, date] = level.reshape(factors, tiles, LANES)
+    counting.wait()
+    largest = count_ref[0]
+    fits = largest <= ROWS
+    wanted = [fits & (largest > 2 * (PAIRS // PARTS) * part) for part in range(PARTS)]
+    for part in range(1, PARTS):
+
+        @pl.when(wanted[part])
+        def _(both=copies[part]):
+            for copy in both:
+                copy.start()
+
+    for copy in copies[0]:
+        copy.wait()
 
     @pl.when(fits)
     def _():
@@ -233,12 +243,13 @@
             return step + 1
 
         step = 0
-        for part, (wanted, both) in enumerate(copies):
-
-            @pl.when(wanted)
-            def _(both=both):
-                for copy in both:
-                    copy.wait()
+        for part, both in enumerate(copies):
+            if part:
+
+                @pl.when(wanted[part])
+                def _(both=both):
+                    for copy in both:
+                        copy.wait()
 
             def more(step, limit=2 * (PAIRS // PARTS) * (part + 1)):
                 last = jnp.maximum(SETS // GROUP - 1 - step, 0)
@@ -250,7 +261,7 @@
         for date in range(dates):
             lines.append(sum(dot_last(ones, p.astype(jnp.bfloat16)) for p in pieces(sum_ref[date]))[:1])
         total = jnp.concatenate(lines + [jnp.zeros((16 - dates, SETS), jnp.float32)], axis=0)
-        moved = moves(place_ref[...])
+        moved = place_ref[...]
         parts = [jnp.dot(p.astype(jnp.bfloat16), moved, preferred_element_type=jnp.float32) for p in pieces(total)]
         out_ref[...] = (parts[0] + (parts[1] + parts[2]))[:dates]
 
@@ -290,12 +301,14 @@
     return pl.pallas_call(
         exposure_kernel,
         out_shape=jax.ShapeDtypeStruct((dates, SETS), jnp.float32),
-        in_specs=[pl.BlockSpec(memory_space=pltpu.SMEM)] + [hbm] * 3 + [vmem] * 4 + [hbm] * 4,
+        in_specs=[hbm] * 4 + [vmem] * 4 + [hbm] * 4,
         out_specs=vmem,
         scratch_shapes=[
+            pltpu.SMEM((SETS,), jnp.int32),
             pltpu.SMEM((PAIRS * SETS,), jnp.int32),
             pltpu.SMEM((PAIRS * 2 * SETS,), jnp.float32),
             pltpu.SMEM((PAIRS * 2 * SETS,), jnp.float32),
+            pltpu.SemaphoreType.DMA,
             pltpu.SemaphoreType.DMA((PARTS, 3)),
             pltpu.VMEM((dates, factors, paths), jnp.float32),
             pltpu.VMEM((factors * dates * (paths // LANES), LANES), jnp.float32),

time: 51.6 us -> 51.4 us (level)
  no operation moved by 1% of the time
where the time goes in v5:
time: 51.4 us; the launch traced here: 51.2 us
  Pallas kernels  18.3 us (36%)
  starting transfers between devices  17.1 us (33%)
  waiting for transfers between devices  10.6 us (21%)
  local copies, waits for them, and re-layouts  3.39 us (7%)
  matrix products  0.8 us (2%)
  other arithmetic  0.78 us (2%)
    ppermute x8, starting transfers between devices, swapped(): return lax.ppermute(part, axis, [(i, i ^ distance) for i in range(size)])  13.5 us
    pallas_call x1, Pallas kernels, exposures(): pl.pallas_call(exposure_kernel, out_shape=jax.ShapeDtypeStruct((dates, SE...  12.5 us
    ppermute x8, waiting for transfers between devices, swapped(): return lax.ppermute(part, axis, [(i, i ^ distance) for i in range(size)])  8.83 us
    pallas_call x1, Pallas kernels, tables(): pl.pallas_call(functools.partial(table_kernel, step), out_shape=(jax.Shap...  5.15 us
    ppermute x1, starting transfers between devices, carried_in(): own = lax.ppermute(half, 'section', pairs)  3.4 us
    unnamed x15, local copies, waits for them, and re-layouts  3.35 us
    ppermute x1, waiting for transfers between devices, carried_in(): other = lax.ppermute(own, 'section', [(i, i ^ 1) for i in range(sections)])  1.33 us
  transfers between devices with their start and end apart: 11, of which 10 were waited for; matrix products, arithmetic and copies ran while one was open for 3% of the time, Pallas kernels for 10%

profile of v5, /device:TPU:0, one launch (start us, length us, event | category | flops | bytes accessed | tf_op | source)
XLA Modules:
  0.0 51.2 jit_solution(9241541874570648025)
XLA Ops:
  0.0 0.0 copy-start.5
  0.0 0.7 %copy-done.5 = s32[8]{0:T(128)S(1)} copy-done((s32[8]{0:T(128)S(1)}, s32[8]{0:T(128)}, u32[]{:S(2)}) %copy-start.5) | copy-done | bytes 56
  0.7 0.0 copy-start
  0.7 0.8 %copy-done = f32[2,1,60,60]{3,1,2,0:T(1,128)S(1)} copy-done((f32[2,1,60,60]{3,1,2,0:T(1,128)S(1)}, f32[2,1,60,60]{3,1,2,0:T(1,128)}, u32[]{:S(2)}) %copy-start) | copy-done | bytes 28824
  1.5 0.6 %pack.1 = f32[60,128]{1,0:T(8,128)S(1)} custom-call(s32[8]{0:T(128)S(1)} %copy-done.5, f32[120,1,60]{2,1,0:T(1,128)S(1)} %bitcast.17), custom_call_target="tpu_custom_call" | custom-call | tf_op jit(solution)/shard_map/pack/pallas_call | solution.py:340
  2.1 4.1 %collective-permute-start = (f32[60,128]{1,0:T(8,128)S(1)}, f32[60,128]{1,0:T(8,128)S(1)}, u32[]{:S(2)}, u32[]{:S(2)}) collective-permute-start(f32[60,128]{1,0:T(8,128)S(1)} %pack.1), channel_id=1, source_target_pairs={{0,4},{1,5},{2,6},{3,7},{4,0},{5,1},{6,2},{7,3},{8,12},{9,13},{10,... | collective-permute-start | bytes 92168 | tf_op jit(solution)/shard_map/ppermute | solution.py:28
  6.2 2.2 %collective-permute-done = f32[60,128]{1,0:T(8,128)S(1)} collective-permute-done((f32[60,128]{1,0:T(8,128)S(1)}, f32[60,128]{1,0:T(8,128)S(1)}, u32[]{:S(2)}, u32[]{:S(2)}) %collective-permute-start) | collective-permute-done | bytes 30752 | tf_op jit(solution)/shard_map/ppermute | solution.py:28
  8.5 2.5 %collective-permute-start.3 = (f32[60,128]{1,0:T(8,128)S(1)}, f32[60,128]{1,0:T(8,128)S(1)}, u32[]{:S(2)}, u32[]{:S(2)}) collective-permute-start(f32[60,128]{1,0:T(8,128)S(1)} %add.46), channel_id=1, source_target_pairs={{0,3},{1,2},{2,1},{3,0},{4,7},{5,6},{6,5},{7,4},{8,11},{9,10},{10,... | collective-permute-start | bytes 92168 | tf_op jit(solution)/shard_map/ppermute | solution.py:28
  11.0 0.7 %collective-permute-start.2 = (f32[60,128]{1,0:T(8,128)S(1)}, f32[60,128]{1,0:T(8,128)S(1)}, u32[]{:S(2)}, u32[]{:S(2)}) collective-permute-start(f32[60,128]{1,0:T(8,128)S(1)} %add.46), channel_id=1, source_target_pairs={{0,2},{1,3},{2,0},{3,1},{4,6},{5,7},{6,4},{7,5},{8,10},{9,11},{10,... | collective-permute-start | bytes 92168 | tf_op jit(solution)/shard_map/ppermute | solution.py:28
  11.7 0.3 collective-permute-start.1
  12.0 1.2 %copy.9 = f32[2,60,1024]{2,1,0:T(8,128)S(1)} copy(f32[2,60,1024]{2,0,1:T(2,128)} %param.8) | data formatting | bytes 983040 | tf_op args[0]
  13.2 0.1 collective-permute-done.3
  13.3 1.6 %collective-permute-done.2 = f32[60,128]{1,0:T(8,128)S(1)} collective-permute-done((f32[60,128]{1,0:T(8,128)S(1)}, f32[60,128]{1,0:T(8,128)S(1)}, u32[]{:S(2)}, u32[]{:S(2)}) %collective-permute-start.2) | collective-permute-done | bytes 30752 | tf_op jit(solution)/shard_map/ppermute | solution.py:28
  14.9 0.7 %collective-permute-done.1 = f32[60,128]{1,0:T(8,128)S(1)} collective-permute-done((f32[60,128]{1,0:T(8,128)S(1)}, f32[60,128]{1,0:T(8,128)S(1)}, u32[]{:S(2)}, u32[]{:S(2)}) %collective-permute-start.1) | collective-permute-done | bytes 30752 | tf_op jit(solution)/shard_map/ppermute | solution.py:28
  15.6 0.4 fusion.6
  16.1 0.1 collective-permute-start.4
  16.1 0.0 copy-start.6
  16.2 0.6 %copy-done.6 = f32[60]{0:T(128)S(1)} copy-done((f32[60]{0:T(128)S(1)}, f32[60]{0:T(128)}, u32[]{:S(2)}) %copy-start.6) | copy-done | bytes 264
  16.8 0.4 convolution_add_fusion.first_ref
  17.2 0.5 collective-permute-done.4
  17.7 0.1 broadcast_add_fusion
  17.7 0.0 copy-start.1
  17.8 0.0 copy-start.2
  17.8 0.0 copy-start.3
  17.8 0.0 copy-start.4
  17.8 3.4 %collective-permute-start.5 = (f32[60,512]{1,0:T(8,128)S(1)}, f32[60,512]{1,0:T(8,128)S(1)}, u32[]{:S(2)}, u32[]{:S(2)}) collective-permute-start(f32[60,512]{1,0:T(8,128)S(1)} %slice_select_fusion), channel_id=1, source_target_pairs={{0,16},{8,24},{1,17},{9,25},{2,18},{10,26},{3,19},{11,27},{4,20},{... | collective-permute-start | bytes 368648 | tf_op jit(solution)/shard_map/ppermute | solution.py:365
  21.2 0.0 copy-done.1
  21.2 0.0 copy-done.2
  21.3 0.0 copy-done.3
  21.3 0.0 copy-done.4
  21.3 5.2 %tables.1 = (s32[16,4,128]{2,1,0:T(4,128)S(1)}, f32[16,8,128]{2,1,0:T(8,128)S(1)}, f32[16,8,128]{2,1,0:T(8,128)S(1)}, bf16[512,512]{1,0:T(8,128)(2,1)S(1)}, s32[1,512]{1,0:T(1,128)S(1)}) custom-call(s32[32,128]{1,0:T(8,128)S(1)} %bitcast.19, s32[32,128]{1,0:T(8,128)S(1)} %bitcast.20, f32[32,128]{1,0:T(8,128)S(1)} %bitcast.21, f32[32,128]{1,0:T(8,128)S(1)} %bitcast.22), custom_call_target="tpu_custom_call" | custom-call | flops 2097152000 | bytes 1048576 | tf_op jit(solution)/shard_map/tables/pallas_call | solution.py:136
  26.4 0.0 collective-permute-done.5
  26.4 0.1 collective-permute-start.6
  26.5 1.3 %collective-permute-done.6 = f32[60,512]{1,0:T(8,128)S(1)} collective-permute-done((f32[60,512]{1,0:T(8,128)S(1)}, f32[60,512]{1,0:T(8,128)S(1)}, u32[]{:S(2)}, u32[]{:S(2)}) %collective-permute-start.6) | collective-permute-done | bytes 122912 | tf_op jit(solution)/shard_map/ppermute | solution.py:367
  27.9 12.5 %exposures.1 = f32[2,512]{1,0:T(2,128)S(1)} custom-call(s32[512]{0:T(512)S(1)} %bitcast.23, s32[8192]{0:T(1024)S(1)} %bitcast.18, f32[16384]{0:T(1024)S(1)} %bitcast.15, f32[16384]{0:T(1024)S(1)} %bitcast.16, bf16[512,512]{1,0:T(8,128)(2,1)S(1)} %get-tuple-element.41.place_ref, f32[60,1024]{1,0:T(8,128)S(1)} %fusion.carry_ref, ...), custom_call_target="tpu_custom_call" | custom-call | tf_op jit(solution)/shard_map/exposures/pallas_call | solution.py:301
  40.4 2.4 %collective-permute-start.7 = (f32[2,512]{1,0:T(2,128)S(1)}, f32[2,512]{1,0:T(2,128)S(1)}, u32[]{:S(2)}, u32[]{:S(2)}) collective-permute-start(f32[2,512]{1,0:T(2,128)S(1)} %exposures.1), channel_id=1, source_target_pairs={{0,4},{1,5},{2,6},{3,7},{4,0},{5,1},{6,2},{7,3},{8,12},{9,13},{10,... | collective-permute-start | bytes 12296 | tf_op jit(solution)/shard_map/ppermute | solution.py:28
  42.8 2.1 %collective-permute-done.7 = f32[2,512]{1,0:T(2,128)S(1)} collective-permute-done((f32[2,512]{1,0:T(2,128)S(1)}, f32[2,512]{1,0:T(2,128)S(1)}, u32[]{:S(2)}, u32[]{:S(2)}) %collective-permute-start.7) | collective-permute-done | bytes 4128 | tf_op jit(solution)/shard_map/ppermute | solution.py:28
  45.0 1.3 %collective-permute-start.10 = (f32[2,512]{1,0:T(2,128)S(1)}, f32[2,512]{1,0:T(2,128)S(1)}, u32[]{:S(2)}, u32[]{:S(2)}) collective-permute-start(f32[2,512]{1,0:T(2,128)S(1)} %add.55), channel_id=1, source_target_pairs={{0,3},{1,2},{2,1},{3,0},{4,7},{5,6},{6,5},{7,4},{8,11},{9,10},{10,... | collective-permute-start | bytes 12296 | tf_op jit(solution)/shard_map/ppermute | solution.py:28
  46.3 0.7 %collective-permute-start.9 = (f32[2,512]{1,0:T(2,128)S(1)}, f32[2,512]{1,0:T(2,128)S(1)}, u32[]{:S(2)}, u32[]{:S(2)}) collective-permute-start(f32[2,512]{1,0:T(2,128)S(1)} %add.55), channel_id=1, source_target_pairs={{0,2},{1,3},{2,0},{3,1},{4,6},{5,7},{6,4},{7,5},{8,10},{9,11},{10,... | collective-permute-start | bytes 12296 | tf_op jit(solution)/shard_map/ppermute | solution.py:28
  46.9 1.5 %collective-permute-start.8 = (f32[2,512]{1,0:T(2,128)S(1)}, f32[2,512]{1,0:T(2,128)S(1)}, u32[]{:S(2)}, u32[]{:S(2)}) collective-permute-start(f32[2,512]{1,0:T(2,128)S(1)} %add.55), channel_id=1, source_target_pairs={{0,1},{1,0},{2,3},{3,2},{4,5},{5,4},{6,7},{7,6},{8,9},{9,8},{10,11... | collective-permute-start | bytes 12296 | tf_op jit(solution)/shard_map/ppermute | solution.py:28
  48.5 1.0 %collective-permute-done.10 = f32[2,512]{1,0:T(2,128)S(1)} collective-permute-done((f32[2,512]{1,0:T(2,128)S(1)}, f32[2,512]{1,0:T(2,128)S(1)}, u32[]{:S(2)}, u32[]{:S(2)}) %collective-permute-start.10) | collective-permute-done | bytes 4128 | tf_op jit(solution)/shard_map/ppermute | solution.py:28
  49.5 0.4 collective-permute-done.9
  49.9 0.7 %collective-permute-done.8 = f32[2,512]{1,0:T(2,128)S(1)} collective-permute-done((f32[2,512]{1,0:T(2,128)S(1)}, f32[2,512]{1,0:T(2,128)S(1)}, u32[]{:S(2)}, u32[]{:S(2)}) %collective-permute-start.8) | collective-permute-done | bytes 4128 | tf_op jit(solution)/shard_map/ppermute | solution.py:28
  50.6 0.6 %add_multiply_fusion = f32[2,512]{1,0:T(2,128)} fusion(f32[2,512]{1,0:T(2,128)S(1)} %collective-permute-done.9, f32[2,512]{1,0:T(2,128)S(1)} %collective-permute-done.10, f32[2,512]{1,0:T(2,128)S(1)} %add.55, f32[2,512]{1,0:T(2,128)S(1)} %collective-permute-done.8), kind=kLoop, calls=%fused_computation.11 | loop fusion | flops 4096 | bytes 20480 | tf_op jit(solution)/shard_map/div | solution.py:400
  (7 shorter events, 0.1 us)
Async XLA Ops:
  0.0 0.7 %copy-start.5 = (s32[8]{0:T(128)S(1)}, s32[8]{0:T(128)}, u32[]{:S(2)}) copy-start(s32[8]{0:T(128)} %owner_ref.1) | copy-start | bytes 100
  0.7 0.8 %copy-start = (f32[2,1,60,60]{3,1,2,0:T(1,128)S(1)}, f32[2,1,60,60]{3,1,2,0:T(1,128)}, u32[]{:S(2)}) copy-start(f32[2,1,60,60]{3,1,2,0:T(1,128)} %param.9) | copy-start | bytes 86404
  2.1 6.4 %collective-permute-start = (f32[60,128]{1,0:T(8,128)S(1)}, f32[60,128]{1,0:T(8,128)S(1)}, u32[]{:S(2)}, u32[]{:S(2)}) collective-permute-start(f32[60,128]{1,0:T(8,128)S(1)} %pack.1), channel_id=1, source_target_pairs={{0,4},{1,5},{2,6},{3,7},{4,0},{5,1},{6,2},{7,3},{8,12},{9,13},{10,... | collective-permute-start | bytes 92168 | tf_op jit(solution)/shard_map/ppermute | solution.py:28
  8.5 4.8 %collective-permute-start.3 = (f32[60,128]{1,0:T(8,128)S(1)}, f32[60,128]{1,0:T(8,128)S(1)}, u32[]{:S(2)}, u32[]{:S(2)}) collective-permute-start(f32[60,128]{1,0:T(8,128)S(1)} %add.46), channel_id=1, source_target_pairs={{0,3},{1,2},{2,1},{3,0},{4,7},{5,6},{6,5},{7,4},{8,11},{9,10},{10,... | collective-permute-start | bytes 92168 | tf_op jit(solution)/shard_map/ppermute | solution.py:28
  11.0 3.9 %collective-permute-start.2 = (f32[60,128]{1,0:T(8,128)S(1)}, f32[60,128]{1,0:T(8,128)S(1)}, u32[]{:S(2)}, u32[]{:S(2)}) collective-permute-start(f32[60,128]{1,0:T(8,128)S(1)} %add.46), channel_id=1, source_target_pairs={{0,2},{1,3},{2,0},{3,1},{4,6},{5,7},{6,4},{7,5},{8,10},{9,11},{10,... | collective-permute-start | bytes 92168 | tf_op jit(solution)/shard_map/ppermute | solution.py:28
  11.7 3.9 %collective-permute-start.1 = (f32[60,128]{1,0:T(8,128)S(1)}, f32[60,128]{1,0:T(8,128)S(1)}, u32[]{:S(2)}, u32[]{:S(2)}) collective-permute-start(f32[60,128]{1,0:T(8,128)S(1)} %add.46), channel_id=1, source_target_pairs={{0,1},{1,0},{2,3},{3,2},{4,5},{5,4},{6,7},{7,6},{8,9},{9,8},{10,11... | collective-permute-start | bytes 92168 | tf_op jit(solution)/shard_map/ppermute | solution.py:28
  16.1 1.6 %collective-permute-start.4 = (f32[60,1024]{1,0:T(8,128)S(1)}, f32[60,1024]{1,0:T(8,128)S(1)}, u32[]{:S(2)}, u32[]{:S(2)}) collective-permute-start(f32[60,1024]{1,0:T(8,128)S(1)} %fusion.6), channel_id=1, source_target_pairs={{0,8},{8,0},{16,24},{24,16},{1,9},{9,1},{17,25},{25,17},{2,10},{10... | collective-permute-start | bytes 737288 | tf_op jit(solution)/shard_map/ppermute | solution.py:360
  16.1 0.7 %copy-start.6 = (f32[60]{0:T(128)S(1)}, f32[60]{0:T(128)}, u32[]{:S(2)}) copy-start(f32[60]{0:T(128)} %param.10) | copy-start | bytes 724
  17.7 3.5 %copy-start.1 = (s32[4096]{0:T(1024)S(1)}, s32[4096]{0:T(1024)}, u32[]{:S(2)}) copy-start(s32[4096]{0:T(1024)} %factor_hbm.1) | copy-start | bytes 49156
  17.8 3.5 %copy-start.2 = (s32[4096]{0:T(1024)S(1)}, s32[4096]{0:T(1024)}, u32[]{:S(2)}) copy-start(s32[4096]{0:T(1024)} %set_hbm.1) | copy-start | bytes 49156
  17.8 3.5 %copy-start.3 = (f32[4096]{0:T(1024)S(1)}, f32[4096]{0:T(1024)}, u32[]{:S(2)}) copy-start(f32[4096]{0:T(1024)} %notional_hbm.1) | copy-start | bytes 49156
  17.8 3.5 %copy-start.4 = (f32[4096]{0:T(1024)S(1)}, f32[4096]{0:T(1024)}, u32[]{:S(2)}) copy-start(f32[4096]{0:T(1024)} %strike_hbm.1) | copy-start | bytes 49156
  17.8 8.6 %collective-permute-start.5 = (f32[60,512]{1,0:T(8,128)S(1)}, f32[60,512]{1,0:T(8,128)S(1)}, u32[]{:S(2)}, u32[]{:S(2)}) collective-permute-start(f32[60,512]{1,0:T(8,128)S(1)} %slice_select_fusion), channel_id=1, source_target_pairs={{0,16},{8,24},{1,17},{9,25},{2,18},{10,26},{3,19},{11,27},{4,20},{... | collective-permute-start | bytes 368648 | tf_op jit(solution)/shard_map/ppermute | solution.py:365
  26.4 1.4 %collective-permute-start.6 = (f32[60,512]{1,0:T(8,128)S(1)}, f32[60,512]{1,0:T(8,128)S(1)}, u32[]{:S(2)}, u32[]{:S(2)}) collective-permute-start(f32[60,512]{1,0:T(8,128)S(1)} %collective-permute-done.5), channel_id=1, source_target_pairs={{0,8},{8,0},{16,24},{24,16},{1,9},{9,1},{17,25},{25,17},{2,10},{10... | collective-permute-start | bytes 368648 | tf_op jit(solution)/shard_map/ppermute | solution.py:367
  40.4 4.6 %collective-permute-start.7 = (f32[2,512]{1,0:T(2,128)S(1)}, f32[2,512]{1,0:T(2,128)S(1)}, u32[]{:S(2)}, u32[]{:S(2)}) collective-permute-start(f32[2,512]{1,0:T(2,128)S(1)} %exposures.1), channel_id=1, source_target_pairs={{0,4},{1,5},{2,6},{3,7},{4,0},{5,1},{6,2},{7,3},{8,12},{9,13},{10,... | collective-permute-start | bytes 12296 | tf_op jit(solution)/shard_map/ppermute | solution.py:28
  45.0 4.5 %collective-permute-start.10 = (f32[2,512]{1,0:T(2,128)S(1)}, f32[2,512]{1,0:T(2,128)S(1)}, u32[]{:S(2)}, u32[]{:S(2)}) collective-permute-start(f32[2,512]{1,0:T(2,128)S(1)} %add.55), channel_id=1, source_target_pairs={{0,3},{1,2},{2,1},{3,0},{4,7},{5,6},{6,5},{7,4},{8,11},{9,10},{10,... | collective-permute-start | bytes 12296 | tf_op jit(solution)/shard_map/ppermute | solution.py:28
  46.3 3.6 %collective-permute-start.9 = (f32[2,512]{1,0:T(2,128)S(1)}, f32[2,512]{1,0:T(2,128)S(1)}, u32[]{:S(2)}, u32[]{:S(2)}) collective-permute-start(f32[2,512]{1,0:T(2,128)S(1)} %add.55), channel_id=1, source_target_pairs={{0,2},{1,3},{2,0},{3,1},{4,6},{5,7},{6,4},{7,5},{8,10},{9,11},{10,... | collective-permute-start | bytes 12296 | tf_op jit(solution)/shard_map/ppermute | solution.py:28
  46.9 3.6 %collective-permute-start.8 = (f32[2,512]{1,0:T(2,128)S(1)}, f32[2,512]{1,0:T(2,128)S(1)}, u32[]{:S(2)}, u32[]{:S(2)}) collective-permute-start(f32[2,512]{1,0:T(2,128)S(1)} %add.55), channel_id=1, source_target_pairs={{0,1},{1,0},{2,3},{3,2},{4,5},{5,4},{6,7},{7,6},{8,9},{9,8},{10,11... | collective-permute-start | bytes 12296 | tf_op jit(solution)/shard_map/ppermute | solution.py:28
